TPU v7x, 32 devices: a whole 2x2x4 slice. The times are simulated.
32 devices in a mesh: rows: 4 (over x, core), cols: 8 (over z, y).
Axes of the slice: x: 2, y: 2, z: 4, core: 2. Of those that a mesh axis runs over, the one named last changes fastest.
Arguments:
- samples: bfloat16 [2048, 65536], P('rows', 'cols'), may hold values from -0.0234375 to 0.0234375
- labels: int32 [2048], P('rows'), may hold values 0 or 1
- weights: float32 [65536], P('cols'), may hold values from -7 to 7, as said below
- hist_s: float32 [16, 65536], P(None, 'cols'), may hold values from -60 to 60
- hist_y: float32 [16, 65536], P(None, 'cols'), may hold values from -480 to 480, as said below
- counter: int32 [1], replicated, may hold values from 0 to 4095
Outputs:
- new_weights: float32 [65536], P('cols')
- gradient: float32 [65536], P('cols')
Inputs may be any that keep to these rules, and one draw needn't show every extreme that they name: weights share a common direction with the rows of hist_s. Each entry of hist_y[j] is a positive multiple of the same entry of hist_s[j], so s_j . y_j > 0.
All inputs are finite; a program needn't handle non-finite values. No bound on the sum of `labels` on one device may be relied on, other than what follows from the above.
Results may differ from a plain program's by a relative error of at most 0.0013.
Values sent between devices are 32-bit elements; how exact they have to be, the bound alone decides.
No kernel may reach another device: no remote copies, remote signals or barrier semaphores. Data moves between devices by JAX's collectives and lax.ppermute only.
A program may use at most 64 MiB of HBM per device.

v0:
```python
import jax
import jax.numpy as jnp
from jax import lax
from jax.sharding import PartitionSpec as P

HIST = 16


penalty = 4.0
step_length = 0.5
highest = lax.Precision.HIGHEST


def row_share(values):
    width = values.shape[-1] // lax.axis_size("rows")
    return lax.dynamic_slice_in_dim(values, lax.axis_index("rows") * width, width, values.ndim - 1)


def quad_form(left, matrix, right):
    return jnp.dot(left, jnp.dot(matrix, right, precision=highest), precision=highest)


def gram_recursion(gram, basis, newest):
    count = 2 * HIST + 1
    places = jnp.arange(count, dtype=jnp.int32)
    select_s = (places == newest).astype(jnp.float32)
    select_y = (places == newest + HIST).astype(jnp.float32)
    gamma = quad_form(select_s, gram, select_y) / quad_form(select_y, gram, select_y)
    weights_of = (places == 2 * HIST).astype(jnp.float32)
    coefs = []
    pairs = []
    for step in range(HIST):
        slot = (newest - step) % HIST
        pick_s = (places == slot).astype(jnp.float32)
        pick_y = (places == slot + HIST).astype(jnp.float32)
        rho = 1.0 / quad_form(pick_s, gram, pick_y)
        coef = rho * quad_form(pick_s, gram, weights_of)
        coefs.append(coef)
        pairs.append((pick_s, pick_y, rho))
        weights_of = weights_of - coef * pick_y
    result_of = gamma * weights_of
    for step in reversed(range(HIST)):
        pick_s, pick_y, rho = pairs[step]
        beta = rho * quad_form(pick_y, gram, result_of)
        result_of = result_of + (coefs[step] - beta) * pick_s
    return jnp.dot(result_of, basis, precision=highest)


def body(samples, labels, weights, hist_s, hist_y, counter):
    margin_part = jnp.dot(samples, weights.astype(jnp.bfloat16), preferred_element_type=jnp.float32)
    margin = lax.psum(margin_part, "cols")
    resid = (jax.nn.sigmoid(margin) - labels.astype(jnp.float32)).astype(jnp.bfloat16)
    total_part = jnp.dot(resid, samples, preferred_element_type=jnp.float32)
    newest = counter[0] % HIST
    total = lax.psum(total_part, "rows")
    gradient = weights + penalty * total
    basis = jnp.concatenate([hist_s, hist_y, gradient[None, :]], axis=0)
    narrow_basis = row_share(basis)
    gram_part = jnp.dot(
        narrow_basis, narrow_basis.T, precision=highest, preferred_element_type=jnp.float32
    )
    gram = lax.psum(gram_part, ("rows", "cols"))
    result = gram_recursion(gram, basis, newest)
    return (weights - step_length * result, gradient)


def solution(mesh):
    in_specs = (P("rows", "cols"), P("rows"), P("cols"), P(None, "cols"), P(None, "cols"), P())
    out_specs = (P("cols"), P("cols"))
    return jax.shard_map(body, mesh=mesh, in_specs=in_specs, out_specs=out_specs, check_vma=False)
```

profile of v0, /device:TPU:0, one launch (start us, length us, event | category | flops | bytes accessed | tf_op | source)
XLA Modules:
  0.0 156.2 jit_solution(8693725162735482173)
XLA Ops:
  0.6 0.8 convert_element_type.8
  1.4 5.6 %fusion.186 = f32[1,512]{1,0:T(1,128)S(1)} fusion(bf16[512,8192]{1,0:T(8,128)(2,1)} %param.6, bf16[8192,1]{0,1:T(2,128)(2,1)S(1)} %reshape.4), kind=kOutput, calls=%fused_computation.303 | convolution fusion | flops 8388608 | bytes 8407040 | tf_op jit(solution)/shard_map/dot_general | solution.py:50
  7.1 23.1 %psum.21 = f32[512]{0:T(512)S(1)} all-reduce(f32[512]{0:T(512)S(1)} %bitcast.507), channel_id=1, replica_groups=mesh['rows'=4,'cols'=8] {'cols'}, use_global_device_ids=true, to_apply=%region_0.0 | all-reduce | flops 512 | bytes 4096 | tf_op jit(solution)/shard_map/psum | solution.py:51
  30.3 4.7 %fusion.187 = f32[1,8192]{1,0:T(1,128)S(1)} fusion(bf16[512,1]{0,1:T(2,128)(2,1)S(1)} %reshape.6, bf16[512,8192]{1,0:T(8,128)(2,1)} %param.6), kind=kOutput, calls=%fused_computation.304 | convolution fusion | flops 8388608 | bytes 8422400 | tf_op jit(solution)/shard_map/dot_general | solution.py:53
  34.9 10.3 %psum.22 = f32[8192]{0:T(1024)S(1)} all-reduce(f32[8192]{0:T(1024)S(1)} %bitcast.505), channel_id=1, replica_groups=mesh['rows'=4,'cols'=8] {'rows'}, use_global_device_ids=true, to_apply=%region_1.2 | all-reduce | flops 8192 | bytes 65536 | tf_op jit(solution)/shard_map/psum | solution.py:55
  45.3 0.1 pad_maximum_fusion
  45.4 0.4 fusion.96
  45.8 37.1 %psum.23 = f32[33,33]{1,0:T(8,128)S(1)} all-reduce(f32[33,33]{1,0:T(8,128)S(1)} %fusion.96), channel_id=1, replica_groups=mesh['rows'=4,'cols'=8] {'rows','cols'}, use_global_device_ids=true, to_apply=%region_2.3 | all-reduce | flops 1089 | bytes 8712 | tf_op jit(solution)/shard_map/psum | solution.py:62
  83.6 0.7 fusion.48
  85.0 0.7 fusion.49
  86.5 0.7 fusion.50
  87.9 0.8 fusion.51
  89.3 0.7 fusion.52
  90.8 0.8 fusion.53
  92.2 0.7 fusion.56
  93.6 0.7 fusion.54
  95.1 0.8 fusion.55
  96.5 0.8 fusion.57
  97.9 0.7 fusion.60
  99.4 0.7 fusion.58
  100.8 0.8 fusion.59
  102.2 0.8 fusion.61
  103.7 0.7 fusion.64
  105.1 0.7 fusion.62
  106.6 0.8 fusion.63
  108.0 0.8 fusion.65
  109.4 0.7 fusion.68
  110.9 0.7 fusion.66
  112.3 0.8 fusion.67
  113.7 0.8 fusion.69
  115.2 0.7 fusion.72
  116.6 0.7 fusion.70
  118.1 0.8 fusion.71
  119.5 0.8 fusion.73
  120.9 0.7 fusion.76
  122.4 0.7 fusion.74
  123.8 0.8 fusion.75
  125.3 0.8 fusion.77
  126.7 0.7 fusion.78
  128.1 0.8 fusion.79
  129.5 0.8 fusion.121
  131.8 0.8 fusion.80
  133.2 0.8 fusion.81
  134.7 0.8 fusion.82
  136.1 0.8 fusion.83
  137.5 0.1 select_add_fusion.11
  137.6 0.8 fusion.84
  139.0 0.8 fusion.85
  140.4 0.1 select_add_fusion.9
  140.4 0.8 fusion.86
  141.9 0.8 fusion.87
  143.3 0.1 select_add_fusion.7
  143.3 0.8 fusion.88
  144.8 0.8 fusion.89
  146.2 0.1 select_add_fusion.5
  146.2 0.8 fusion.90
  147.6 0.8 fusion.91
  149.1 0.1 select_add_fusion.3
  149.1 0.8 fusion.92
  150.6 0.8 fusion.93
  152.0 0.8 fusion.94
  153.4 0.8 fusion.95
  154.8 0.7 fusion.124
  155.5 0.6 multiply_subtract_fusion
  (23 shorter events, 0.3 us)
Async XLA Ops:
  1.4 28.8 %copy-start.4 = (s32[512]{0:T(512)S(1)}, s32[512]{0:T(512)}, u32[]{:S(2)}) copy-start(s32[512]{0:T(512)} %param.7) | copy-start | bytes 6148
  30.2 15.0 %copy-start.2 = (f32[8192]{0:T(1024)S(1)}, f32[8192]{0:T(1024)}, u32[]{:S(2)}) copy-start(f32[8192]{0:T(1024)} %param.8) | copy-start | bytes 98308
  30.3 15.0 %copy-start = (f32[16,8192]{1,0:T(8,128)S(1)}, f32[16,8192]{1,0:T(8,128)}, u32[]{:S(2)}) copy-start(f32[16,8192]{1,0:T(8,128)} %param.10) | copy-start | bytes 1572868
  30.3 15.0 %copy-start.1 = (f32[16,8192]{1,0:T(8,128)S(1)}, f32[16,8192]{1,0:T(8,128)}, u32[]{:S(2)}) copy-start(f32[16,8192]{1,0:T(8,128)} %param.9) | copy-start | bytes 1572868
  45.2 109.5 %copy-start.3 = (f32[8192]{0:T(1024)}, f32[8192]{0:T(1024)S(1)}, u32[]{:S(2)}) copy-start(f32[8192]{0:T(1024)S(1)} %multiply_add_fusion) | copy-start | bytes 98308
where the time goes:
time: 158 us; the launch traced here: 156 us
  blocking collectives  70.5 us (45%)
  matrix products  48.3 us (31%)
  between operations  35.2 us (22%)
  other arithmetic  2.05 us (1%)
    psum x1, blocking collectives, body(): gram = lax.psum(gram_part, ('rows', 'cols'))  37.1 us
    dot_general x49, matrix products, quad_form(): jnp.dot(matrix, right, precision=highest)  36.8 us
    psum x1, blocking collectives, body(): margin = lax.psum(margin_part, 'cols')  23.1 us
    psum x1, blocking collectives, body(): total = lax.psum(total_part, 'rows')  10.3 us
    dot_general x1, matrix products, body(): jnp.dot(samples, weights.astype(jnp.bfloat16), preferred_element_type=jnp...  5.64 us
    dot_general x1, matrix products, body(): total_part = jnp.dot(resid, samples, preferred_element_type=jnp.float32)  4.66 us

commit v1 on v0

v1 whole, which is shorter than its diff:
```python
import jax
import jax.numpy as jnp
from jax import lax
from jax.experimental import pallas as pl
from jax.experimental.pallas import tpu as pltpu
from jax.sharding import PartitionSpec as P

HIST = 16
LANES = 128
TAIL = 8

penalty = 4.0
step_length = 0.5
highest = lax.Precision.HIGHEST

ANY = pl.BlockSpec(memory_space=pl.ANY)
VM = pl.BlockSpec(memory_space=pltpu.VMEM)
SM = pl.BlockSpec(memory_space=pltpu.SMEM)
SMALL_GRANT = pltpu.CompilerParams(vmem_limit_bytes=16 << 20)


def pieces(values):
    out = []
    for _ in range(3):
        part = values.astype(jnp.bfloat16)
        out.append(part)
        values = values - part.astype(jnp.float32)
    return out


def contract_last(left, right):
    dims = (((1,), (1,)), ((), ()))
    return lax.dot_general(left, right, dims, preferred_element_type=jnp.float32)


def first_kernel(chunks, x_hbm, w_hbm, s_hbm, y_hbm, x_out, w_out, s_out, y_out, pay, z_buf, small_sem, x_sem):
    rows, width = x_out.shape
    step = width // chunks
    smalls = [
        pltpu.make_async_copy(src, dst, small_sem.at[k])
        for k, (src, dst) in enumerate(((w_hbm, w_out), (s_hbm, s_out), (y_hbm, y_out)))
    ]
    bigs = [
        pltpu.make_async_copy(
            x_hbm.at[:, pl.ds(c * step, step)], x_out.at[:, pl.ds(c * step, step)], x_sem.at[c]
        )
        for c in range(chunks)
    ]
    for copy in smalls + bigs:
        copy.start()
    for copy in smalls:
        copy.wait()
    for c in range(chunks):
        cut = pl.ds(c * step, step)
        both = jnp.concatenate([s_out[:, cut], y_out[:, cut]], axis=0)
        for k, part in enumerate(pieces(both)):
            z_buf[2 * HIST * k : 2 * HIST * (k + 1), cut] = part
        w_parts = pieces(w_out[:, cut])
        place = lax.broadcasted_iota(jnp.int32, (HIST, step), 0)
        w_rows = jnp.zeros((HIST, step), jnp.float32)
        for k, part in enumerate(w_parts):
            w_rows = jnp.where(place == k, part.astype(jnp.float32), w_rows)
        z_buf[6 * HIST :, cut] = w_rows.astype(jnp.bfloat16)
    with_x = jnp.zeros((7 * HIST, rows), jnp.float32)
    with_z = jnp.zeros((7 * HIST, 7 * HIST), jnp.float32)
    for c in range(chunks):
        cut = pl.ds(c * step, step)
        z_part = z_buf[:, cut]
        with_z = with_z + contract_last(z_part, z_part)
    for c in range(chunks):
        cut = pl.ds(c * step, step)
        z_part = z_buf[:, cut]
        bigs[c].wait()
        with_x = with_x + contract_last(z_part, x_out[:, cut])
    both = 2 * HIST
    pay[:both, :] = with_x[:both] + (with_x[both : 2 * both] + with_x[2 * both : 3 * both])
    pay[both:, :] = jnp.zeros((TAIL, rows), jnp.float32)
    pay[both : both + 1, :] = with_x[3 * both : 3 * both + 1]
    gram = with_z[:both] + (with_z[both : 2 * both] + with_z[2 * both : 3 * both])
    of_y = gram[:, HIST:both] + (gram[:, 3 * HIST : 4 * HIST] + gram[:, 5 * HIST : 6 * HIST])
    at = 6 * HIST
    of_w = gram[:, at : at + 1] + (gram[:, at + 1 : at + 2] + gram[:, at + 2 : at + 3])
    wide = jnp.concatenate([of_y[:HIST], of_y[HIST:], of_w[:HIST], of_w[HIST:]], axis=1)
    for k in range(4):
        pay[both + 4 : both + 8, LANES * k : LANES * k + both + 2] = wide[4 * k : 4 * k + 4]


def second_kernel(chunks, x_ref, own, got, label_ref, pay, gram):
    both = 2 * HIST
    rows, width = x_ref.shape
    step = width // chunks
    tail = own[both:, :] + got[both:, :]
    gram[...] = tail
    margin = tail[0:1, :]
    resid = (jax.nn.sigmoid(margin) - label_ref[...].astype(jnp.float32)).astype(jnp.bfloat16)
    for c in range(chunks):
        cut = pl.ds(c * step, step)
        pay[:, cut] = jnp.dot(resid, x_ref[:, cut], preferred_element_type=jnp.float32)
    cross = (own[:both, :] + got[:both, :]) * resid.astype(jnp.float32)
    column = jnp.sum(cross, axis=1, keepdims=True)
    row_at = lax.broadcasted_iota(jnp.int32, (both, LANES), 0)
    lane_at = lax.broadcasted_iota(jnp.int32, (both, LANES), 1)
    pay[:, width:] = jnp.sum(jnp.where(row_at == lane_at, column, 0.0), axis=0, keepdims=True)


def to_column(row, count):
    row_at = lax.broadcasted_iota(jnp.int32, (count, count), 0)
    lane_at = lax.broadcasted_iota(jnp.int32, (count, count), 1)
    return jnp.sum(jnp.where(row_at == lane_at, row, 0.0), axis=1, keepdims=True)


def solve_kernel(counter, gram, out):
    newest = lax.rem(counter[0], HIST)
    wide = jnp.concatenate(
        [gram[4:8, LANES * k : LANES * (k + 1)] for k in range(4)], axis=0
    )
    sy = wide[:, :HIST]
    yy = wide[:, HIST : 2 * HIST]
    row_at = lax.broadcasted_iota(jnp.int32, (HIST, HIST), 0)
    lane_at = lax.broadcasted_iota(jnp.int32, (HIST, HIST), 1)
    row_age = lax.rem(newest - row_at + HIST, HIST)
    lane_age = lax.rem(newest - lane_at + HIST, HIST)
    eye = row_at == lane_at
    diag_col = jnp.sum(jnp.where(eye, sy, 0.0), axis=1, keepdims=True)
    rho_col = 1.0 / diag_col
    strict = jnp.where(lane_age < row_age, sy, 0.0) * rho_col
    rest = jnp.where(eye, rho_col, 0.0)
    for age in range(HIST - 1):
        column = jnp.sum(jnp.where(lane_age == age, strict, 0.0), axis=1, keepdims=True)
        row = jnp.sum(jnp.where(row_age == age, rest, 0.0), axis=0, keepdims=True)
        rest = rest - column * row
    at_new = jnp.logical_and(row_at == newest, lane_at == newest)
    top = jnp.sum(jnp.sum(jnp.where(at_new, sy, 0.0), axis=1, keepdims=True), axis=0, keepdims=True)
    low = jnp.sum(jnp.sum(jnp.where(at_new, yy, 0.0), axis=1, keepdims=True), axis=0, keepdims=True)
    gamma = top / low
    middle = jnp.where(eye, diag_col, 0.0) + gamma * yy
    right = jnp.dot(middle, rest, precision=highest, preferred_element_type=jnp.float32)
    flip = (((0,), (0,)), ((), ()))
    corner = lax.dot_general(rest, right, flip, precision=highest, preferred_element_type=jnp.float32)
    turned = lax.dot_general(
        rest, jnp.where(eye, 1.0, 0.0), flip, precision=highest, preferred_element_type=jnp.float32
    )
    out[...] = jnp.zeros(out.shape, jnp.float32)
    out[0:HIST, 0:HIST] = corner
    out[0:HIST, HIST : 2 * HIST] = -gamma * turned
    out[HIST : 2 * HIST, 0:HIST] = -gamma * rest
    ones = jnp.ones((1, LANES), jnp.float32)
    out[2 * HIST : 2 * HIST + 1, :] = gamma * ones
    w_col = jnp.concatenate([wide[:, 2 * HIST : 2 * HIST + 1], wide[:, 2 * HIST + 1 : 2 * HIST + 2]], axis=0)
    big_row = lax.broadcasted_iota(jnp.int32, (2 * HIST, LANES), 0)
    big_lane = lax.broadcasted_iota(jnp.int32, (2 * HIST, LANES), 1)
    out[2 * HIST + 1 : 2 * HIST + 2, :] = jnp.sum(
        jnp.where(big_row == big_lane, w_col, 0.0), axis=0, keepdims=True
    )


def last_kernel(chunks, count, *refs):
    parts = refs[:count]
    coef_ref, w_ref, s_ref, y_ref, new_ref, grad_ref = refs[count:]
    both = 2 * HIST
    width = w_ref.shape[1]
    step = width // chunks

    def summed(cut):
        level = [p[:, cut] for p in parts]
        while len(level) > 1:
            level = [level[k] + level[k + 1] for k in range(0, len(level), 2)]
        return level[0]

    dots = coef_ref[both + 1 : both + 2, :] + penalty * summed(pl.ds(width, LANES))
    gamma = coef_ref[both : both + 1, 0:1]
    coef = jnp.sum(coef_ref[:both, :] * dots, axis=1, keepdims=True)
    for c in range(chunks):
        cut = pl.ds(c * step, step)
        weights = w_ref[:, cut]
        gradient = weights + penalty * summed(cut)
        grad_ref[:, cut] = gradient
        mixed = coef[:HIST] * s_ref[:, cut] + coef[HIST:] * y_ref[:, cut]
        turn = gamma * gradient + jnp.sum(mixed, axis=0, keepdims=True)
        new_ref[:, cut] = weights - step_length * turn


def hop(values, axis, bit):
    size = lax.axis_size(axis)
    return lax.ppermute(values, axis, [(k, k ^ bit) for k in range(size)])


def body(samples, labels, weights, hist_s, hist_y, counter):
    rows, width = samples.shape
    both = 2 * HIST
    f32 = jnp.float32
    chunks = 8
    w_row = weights.reshape(1, width)
    x_in, w_in, s_in, y_in, pay = pl.pallas_call(
        lambda *refs: first_kernel(chunks, *refs),
        in_specs=[ANY] * 4,
        out_specs=[VM] * 5,
        out_shape=[
            pltpu.VMEM((rows, width), jnp.bfloat16),
            pltpu.VMEM((1, width), f32),
            pltpu.VMEM((HIST, width), f32),
            pltpu.VMEM((HIST, width), f32),
            pltpu.VMEM((both + TAIL, rows), f32),
        ],
        scratch_shapes=[
            pltpu.VMEM((7 * HIST, width), jnp.bfloat16),
            pltpu.SemaphoreType.DMA((3,)),
            pltpu.SemaphoreType.DMA((chunks,)),
        ],
        compiler_params=SMALL_GRANT,
        name="load_and_project",
    )(samples, w_row, hist_s, hist_y)

    bit = 1
    cols = lax.axis_size("cols")
    while 2 * bit < cols:
        pay = pay + hop(pay, "cols", bit)
        bit *= 2
    got = hop(pay, "cols", bit) if cols > 1 else jnp.zeros_like(pay)

    part, gram = pl.pallas_call(
        lambda *refs: second_kernel(chunks, *refs),
        in_specs=[VM] * 4,
        out_specs=[VM] * 2,
        out_shape=[pltpu.VMEM((1, width + LANES), f32), pltpu.VMEM((TAIL, rows), f32)],
        compiler_params=SMALL_GRANT,
        name="residual_and_gradient",
    )(x_in, pay, got, labels.reshape(1, rows))

    coefs = pl.pallas_call(
        solve_kernel,
        in_specs=[SM, VM],
        out_specs=VM,
        out_shape=pltpu.VMEM((both + TAIL, LANES), f32),
        compiler_params=SMALL_GRANT,
        name="solve_history",
    )(counter, gram)

    size = lax.axis_size("rows")
    bit = size // 2
    while bit > 2:
        part = part + hop(part, "rows", bit)
        bit //= 2
    parts = [part] + [hop(part, "rows", k) for k in range(1, min(size, 4))]

    new_w, grad = pl.pallas_call(
        lambda *refs: last_kernel(chunks, len(parts), *refs),
        in_specs=[VM] * (len(parts) + 4),
        out_specs=[VM] * 2,
        out_shape=[jax.ShapeDtypeStruct((1, width), f32)] * 2,
        compiler_params=SMALL_GRANT,
        name="direction_and_update",
    )(*parts, coefs, w_in, s_in, y_in)
    return new_w.reshape(width), grad.reshape(width)


def solution(mesh):
    in_specs = (P("rows", "cols"), P("rows"), P("cols"), P(None, "cols"), P(None, "cols"), P())
    out_specs = (P("cols"), P("cols"))
    return jax.shard_map(body, mesh=mesh, in_specs=in_specs, out_specs=out_specs, check_vma=False)
```

time: 158 us -> 38.6 us (0.24)
  blocking collectives: 70.5 us -> 0 us
  matrix products: 48.3 us -> 0 us
  between operations: 35.2 us -> 1.32 us
  Pallas kernels: 0 us -> 11.1 us
  starting transfers between devices: 0 us -> 10.2 us
  waiting for transfers between devices: 0 us -> 9.36 us
  local copies, waits for them, and re-layouts: 0.06 us -> 6.22 us
  other arithmetic: 2.05 us -> 0.03 us
    psum x3 -> x0, blocking collectives: 70.5 us -> none  [the longest x1 37.1 us: body(): gram = lax.psum(gram_part, ('rows', 'cols'))]
    dot_general x53 -> x0, matrix products: 48.3 us -> none  [the longest x49 36.8 us: quad_form(): jnp.dot(matrix, right, precision=highest)]
    pallas_call x0 -> x4, Pallas kernels: none -> 11.1 us  [the longest x1 8.44 us: body(): pl.pallas_call(lambda *refs: first_kernel(chunks, *refs), in_specs=[ANY]...]
    ppermute x0 -> x6, starting transfers between devices: none -> 10.2 us  [hop(): return lax.ppermute(values, axis, [(k, k ^ bit) for k in range(size)])]
    ppermute x0 -> x6, waiting for transfers between devices: none -> 9.36 us  [hop(): return lax.ppermute(values, axis, [(k, k ^ bit) for k in range(size)])]
    unnamed x10, local copies, waits for them, and re-layouts: 0.03 us -> 6.22 us
  transfers between devices with their start and end apart: 0 -> 6, of which waited for: 0 -> 5; matrix products, arithmetic and copies ran while one was open for 0% -> 0% of each run, Pallas kernels for 0% -> 2%
where the time goes in v1:
time: 38.6 us; the launch traced here: 38.2 us
  Pallas kernels  11.1 us (29%)
  starting transfers between devices  10.2 us (26%)
  waiting for transfers between devices  9.36 us (24%)
  local copies, waits for them, and re-layouts  6.22 us (16%)
  between operations  1.32 us (3%)
    ppermute x6, starting transfers between devices, hop(): return lax.ppermute(values, axis, [(k, k ^ bit) for k in range(size)])  10.2 us
    ppermute x6, waiting for transfers between devices, hop(): return lax.ppermute(values, axis, [(k, k ^ bit) for k in range(size)])  9.36 us
    pallas_call x1, Pallas kernels, body(): pl.pallas_call(lambda *refs: first_kernel(chunks, *refs), in_specs=[ANY]...  8.44 us
    unnamed x10, local copies, waits for them, and re-layouts  6.22 us
    pallas_call x1, Pallas kernels, body(): pl.pallas_call(lambda *refs: second_kernel(chunks, *refs), in_specs=[VM]...  1.2 us
    pallas_call x1, Pallas kernels, body(): pl.pallas_call(lambda *refs: last_kernel(chunks, len(parts), *refs), in_s...  0.87 us
  transfers between devices with their start and end apart: 6, of which 5 were waited for; matrix products, arithmetic and copies ran while one was open for 0% of the time, Pallas kernels for 2%

profile of v1, /device:TPU:0, one launch (start us, length us, event | category | flops | bytes accessed | tf_op | source)
XLA Modules:
  0.0 38.2 jit_solution(12119292588280091396)
XLA Ops:
  0.6 0.0 copy-start
  0.6 3.4 %copy-done = bf16[512,8192]{1,0:T(8,128)(2,1)S(1)} copy-done((bf16[512,8192]{1,0:T(8,128)(2,1)S(1)}, bf16[512,8192]{1,0:T(8,128)(2,1)}, u32[]{:S(2)}) %copy-start) | copy-done | bytes 8388632
  4.0 0.0 copy-start.1
  4.0 1.0 %copy-done.1 = f32[16,8192]{1,0:T(8,128)S(1)} copy-done((f32[16,8192]{1,0:T(8,128)S(1)}, f32[16,8192]{1,0:T(8,128)}, u32[]{:S(2)}) %copy-start.1) | copy-done | bytes 524312
  5.1 0.0 copy-start.2
  5.1 1.0 %copy-done.2 = f32[16,8192]{1,0:T(8,128)S(1)} copy-done((f32[16,8192]{1,0:T(8,128)S(1)}, f32[16,8192]{1,0:T(8,128)}, u32[]{:S(2)}) %copy-start.2) | copy-done | bytes 524312
  6.1 0.0 copy-start.3
  6.1 0.8 %copy-done.3 = f32[8192]{0:T(1024)S(1)} copy-done((f32[8192]{0:T(1024)S(1)}, f32[8192]{0:T(1024)}, u32[]{:S(2)}) %copy-start.3) | copy-done | bytes 32792
  6.9 0.0 copy-start.4
  6.9 8.4 %load_and_project.1 = (bf16[512,8192]{1,0:T(8,128)(2,1)S(1)}, f32[1,8192]{1,0:T(1,128)S(1)}, f32[16,8192]{1,0:T(8,128)S(1)}, f32[16,8192]{1,0:T(8,128)S(1)}, f32[40,512]{1,0:T(8,128)S(1)}) custom-call(bf16[512,8192]{1,0:T(8,128)(2,1)S(1)} %copy-done, f32[1,8192]{1,0:T(1,128)S(1)} %bitcast.4, f32[16,8192]{1,0:T(8,128)S(1)} %copy-done.1, f32[16,8192]{1,0:T(8,128)S(1)} %copy-done.2), custom_call_target="tpu_custom_call" | custom-call | tf_op jit(solution)/shard_map/load_and_project/pallas_call | solution.py:194
  15.3 3.1 %collective-permute-start = (f32[40,512]{1,0:T(8,128)S(1)}, f32[40,512]{1,0:T(8,128)S(1)}, u32[]{:S(2)}, u32[]{:S(2)}) collective-permute-start(f32[40,512]{1,0:T(8,128)S(1)} %get-tuple-element.12), channel_id=1, source_target_pairs={{0,1},{1,0},{2,3},{3,2},{4,5},{5,4},{6,7},{7,6},{8,9},{9,8},{10,11... | collective-permute-start | bytes 245768 | tf_op jit(solution)/shard_map/ppermute | solution.py:185
  18.4 2.4 %collective-permute-done = f32[40,512]{1,0:T(8,128)S(1)} collective-permute-done((f32[40,512]{1,0:T(8,128)S(1)}, f32[40,512]{1,0:T(8,128)S(1)}, u32[]{:S(2)}, u32[]{:S(2)}) %collective-permute-start) | collective-permute-done | bytes 81952 | tf_op jit(solution)/shard_map/ppermute | solution.py:185
  20.8 2.1 %collective-permute-start.1 = (f32[40,512]{1,0:T(8,128)S(1)}, f32[40,512]{1,0:T(8,128)S(1)}, u32[]{:S(2)}, u32[]{:S(2)}) collective-permute-start(f32[40,512]{1,0:T(8,128)S(1)} %add.6), channel_id=1, source_target_pairs={{0,2},{1,3},{2,0},{3,1},{4,6},{5,7},{6,4},{7,5},{8,10},{9,11},{10,... | collective-permute-start | bytes 245768 | tf_op jit(solution)/shard_map/ppermute | solution.py:185
  22.9 2.4 %collective-permute-done.1 = f32[40,512]{1,0:T(8,128)S(1)} collective-permute-done((f32[40,512]{1,0:T(8,128)S(1)}, f32[40,512]{1,0:T(8,128)S(1)}, u32[]{:S(2)}, u32[]{:S(2)}) %collective-permute-start.1) | collective-permute-done | bytes 81952 | tf_op jit(solution)/shard_map/ppermute | solution.py:185
  25.4 3.1 %collective-permute-start.2 = (f32[40,512]{1,0:T(8,128)S(1)}, f32[40,512]{1,0:T(8,128)S(1)}, u32[]{:S(2)}, u32[]{:S(2)}) collective-permute-start(f32[40,512]{1,0:T(8,128)S(1)} %add.7.refs_1_), channel_id=1, source_target_pairs={{0,4},{1,5},{2,6},{3,7},{4,0},{5,1},{6,2},{7,3},{8,12},{9,13},{10,... | collective-permute-start | bytes 245768 | tf_op jit(solution)/shard_map/ppermute | solution.py:185
  28.5 2.4 %collective-permute-done.2.refs_2_ = f32[40,512]{1,0:T(8,128)S(1)} collective-permute-done((f32[40,512]{1,0:T(8,128)S(1)}, f32[40,512]{1,0:T(8,128)S(1)}, u32[]{:S(2)}, u32[]{:S(2)}) %collective-permute-start.2) | collective-permute-done | bytes 81952 | tf_op jit(solution)/shard_map/ppermute | solution.py:185
  30.9 0.0 copy-done.4
  30.9 1.2 %residual_and_gradient.1 = (f32[1,8320]{1,0:T(1,128)S(1)}, f32[8,512]{1,0:T(8,128)S(1)}) custom-call(bf16[512,8192]{1,0:T(8,128)(2,1)S(1)} %get-tuple-element.11.refs_0_, f32[40,512]{1,0:T(8,128)S(1)} %add.7.refs_1_, f32[40,512]{1,0:T(8,128)S(1)} %collective-permute-done.2.refs_2_, s32[1,512]{1,0:T(1,128)S(1)} %bitcast.5), custom_call_target="tpu_custom_call" | custom-call | tf_op jit(solution)/shard_map/residual_and_gradient/pallas_call | solution.py:221
  32.1 0.0 collective-permute-start.3
  32.1 1.9 %collective-permute-start.4 = (f32[1,8320]{1,0:T(1,128)S(1)}, f32[1,8320]{1,0:T(1,128)S(1)}, u32[]{:S(2)}, u32[]{:S(2)}) collective-permute-start(f32[1,8320]{1,0:T(1,128)S(1)} %get-tuple-element.13.refs_0_), channel_id=1, source_target_pairs={{0,16},{8,24},{16,0},{24,8},{1,17},{9,25},{17,1},{25,9},{2,18},{10... | collective-permute-start | bytes 99848 | tf_op jit(solution)/shard_map/ppermute | solution.py:185
  34.0 0.1 collective-permute-start.5
  34.7 0.6 %solve_history.1.refs_4_ = f32[40,128]{1,0:T(8,128)S(1)} custom-call(s32[1]{0:T(128)S(6)} %copy.8.counter, f32[8,512]{1,0:T(8,128)S(1)} %get-tuple-element.14.gram), custom_call_target="tpu_custom_call" | custom-call | tf_op jit(solution)/shard_map/solve_history/pallas_call | solution.py:230
  35.3 0.0 collective-permute-done.3.refs_1_
  35.3 0.8 %collective-permute-done.4.refs_2_ = f32[1,8320]{1,0:T(1,128)S(1)} collective-permute-done((f32[1,8320]{1,0:T(1,128)S(1)}, f32[1,8320]{1,0:T(1,128)S(1)}, u32[]{:S(2)}, u32[]{:S(2)}) %collective-permute-start.4) | collective-permute-done | bytes 33312 | tf_op jit(solution)/shard_map/ppermute | solution.py:185
  36.1 1.3 %collective-permute-done.5.refs_3_ = f32[1,8320]{1,0:T(1,128)S(1)} collective-permute-done((f32[1,8320]{1,0:T(1,128)S(1)}, f32[1,8320]{1,0:T(1,128)S(1)}, u32[]{:S(2)}, u32[]{:S(2)}) %collective-permute-start.5) | collective-permute-done | bytes 33312 | tf_op jit(solution)/shard_map/ppermute | solution.py:185
  37.4 0.9 %direction_and_update.1 = (f32[1,8192]{1,0:T(1,128)}, f32[1,8192]{1,0:T(1,128)}) custom-call(f32[1,8320]{1,0:T(1,128)S(1)} %get-tuple-element.13.refs_0_, f32[1,8320]{1,0:T(1,128)S(1)} %collective-permute-done.3.refs_1_, f32[1,8320]{1,0:T(1,128)S(1)} %collective-permute-done.4.refs_2_, f32[1,8320]{1,0:T(1,128)S(1)} %collective-permute-done.5.refs_3_, ...), custom_call_target="tpu_custom_call" | custom-call | tf_op jit(solution)/shard_map/direction_and_update/pallas_call | solution.py:246
  (2 shorter events, 0.0 us)
Async XLA Ops:
  0.6 3.4 %copy-start = (bf16[512,8192]{1,0:T(8,128)(2,1)S(1)}, bf16[512,8192]{1,0:T(8,128)(2,1)}, u32[]{:S(2)}) copy-start(bf16[512,8192]{1,0:T(8,128)(2,1)} %refs_0_.1) | copy-start | bytes 25165828
  4.0 1.0 %copy-start.1 = (f32[16,8192]{1,0:T(8,128)S(1)}, f32[16,8192]{1,0:T(8,128)}, u32[]{:S(2)}) copy-start(f32[16,8192]{1,0:T(8,128)} %refs_2_.1) | copy-start | bytes 1572868
  5.1 1.0 %copy-start.2 = (f32[16,8192]{1,0:T(8,128)S(1)}, f32[16,8192]{1,0:T(8,128)}, u32[]{:S(2)}) copy-start(f32[16,8192]{1,0:T(8,128)} %refs_3_.1) | copy-start | bytes 1572868
  6.1 0.8 %copy-start.3 = (f32[8192]{0:T(1024)S(1)}, f32[8192]{0:T(1024)}, u32[]{:S(2)}) copy-start(f32[8192]{0:T(1024)} %param.8) | copy-start | bytes 98308
  6.9 24.1 %copy-start.4 = (s32[512]{0:T(512)S(1)}, s32[512]{0:T(512)}, u32[]{:S(2)}) copy-start(s32[512]{0:T(512)} %param.7) | copy-start | bytes 6148
  15.3 5.5 %collective-permute-start = (f32[40,512]{1,0:T(8,128)S(1)}, f32[40,512]{1,0:T(8,128)S(1)}, u32[]{:S(2)}, u32[]{:S(2)}) collective-permute-start(f32[40,512]{1,0:T(8,128)S(1)} %get-tuple-element.12), channel_id=1, source_target_pairs={{0,1},{1,0},{2,3},{3,2},{4,5},{5,4},{6,7},{7,6},{8,9},{9,8},{10,11... | collective-permute-start | bytes 245768 | tf_op jit(solution)/shard_map/ppermute | solution.py:185
  20.8 4.5 %collective-permute-start.1 = (f32[40,512]{1,0:T(8,128)S(1)}, f32[40,512]{1,0:T(8,128)S(1)}, u32[]{:S(2)}, u32[]{:S(2)}) collective-permute-start(f32[40,512]{1,0:T(8,128)S(1)} %add.6), channel_id=1, source_target_pairs={{0,2},{1,3},{2,0},{3,1},{4,6},{5,7},{6,4},{7,5},{8,10},{9,11},{10,... | collective-permute-start | bytes 245768 | tf_op jit(solution)/shard_map/ppermute | solution.py:185
  25.4 5.5 %collective-permute-start.2 = (f32[40,512]{1,0:T(8,128)S(1)}, f32[40,512]{1,0:T(8,128)S(1)}, u32[]{:S(2)}, u32[]{:S(2)}) collective-permute-start(f32[40,512]{1,0:T(8,128)S(1)} %add.7.refs_1_), channel_id=1, source_target_pairs={{0,4},{1,5},{2,6},{3,7},{4,0},{5,1},{6,2},{7,3},{8,12},{9,13},{10,... | collective-permute-start | bytes 245768 | tf_op jit(solution)/shard_map/ppermute | solution.py:185
  32.1 3.2 %collective-permute-start.3 = (f32[1,8320]{1,0:T(1,128)S(1)}, f32[1,8320]{1,0:T(1,128)S(1)}, u32[]{:S(2)}, u32[]{:S(2)}) collective-permute-start(f32[1,8320]{1,0:T(1,128)S(1)} %get-tuple-element.13.refs_0_), channel_id=1, source_target_pairs={{0,8},{8,0},{16,24},{24,16},{1,9},{9,1},{17,25},{25,17},{2,10},{10... | collective-permute-start | bytes 99848 | tf_op jit(solution)/shard_map/ppermute | solution.py:185
  32.1 4.0 %collective-permute-start.4 = (f32[1,8320]{1,0:T(1,128)S(1)}, f32[1,8320]{1,0:T(1,128)S(1)}, u32[]{:S(2)}, u32[]{:S(2)}) collective-permute-start(f32[1,8320]{1,0:T(1,128)S(1)} %get-tuple-element.13.refs_0_), channel_id=1, source_target_pairs={{0,16},{8,24},{16,0},{24,8},{1,17},{9,25},{17,1},{25,9},{2,18},{10... | collective-permute-start | bytes 99848 | tf_op jit(solution)/shard_map/ppermute | solution.py:185
  34.0 3.4 %collective-permute-start.5 = (f32[1,8320]{1,0:T(1,128)S(1)}, f32[1,8320]{1,0:T(1,128)S(1)}, u32[]{:S(2)}, u32[]{:S(2)}) collective-permute-start(f32[1,8320]{1,0:T(1,128)S(1)} %get-tuple-element.13.refs_0_), channel_id=1, source_target_pairs={{0,24},{8,16},{16,8},{24,0},{1,25},{9,17},{17,9},{25,1},{2,26},{10... | collective-permute-start | bytes 99848 | tf_op jit(solution)/shard_map/ppermute | solution.py:185

commit v2 on v1

--- a/solution.py
+++ b/solution.py
@@ -13,7 +13,7 @@
 step_length = 0.5
 highest = lax.Precision.HIGHEST
 
-ANY = pl.BlockSpec(memory_space=pl.ANY)
+HBM = pl.BlockSpec(memory_space=pltpu.HBM)
 VM = pl.BlockSpec(memory_space=pltpu.VMEM)
 SM = pl.BlockSpec(memory_space=pltpu.SMEM)
 SMALL_GRANT = pltpu.CompilerParams(vmem_limit_bytes=16 << 20)
@@ -33,56 +33,70 @@
     return lax.dot_general(left, right, dims, preferred_element_type=jnp.float32)
 
 
-def first_kernel(chunks, x_hbm, w_hbm, s_hbm, y_hbm, x_out, w_out, s_out, y_out, pay, z_buf, small_sem, x_sem):
+def first_kernel(blocks, place_ref, x_hbm, w_hbm, s_hbm, y_hbm, pay, x_out, w_out, s_out, y_out, acc, z_buf, sem):
     rows, width = x_out.shape
-    step = width // chunks
+    both = 2 * HIST
+    step = width // sum(blocks)
     smalls = [
-        pltpu.make_async_copy(src, dst, small_sem.at[k])
+        pltpu.make_async_copy(src, dst, sem.at[k])
         for k, (src, dst) in enumerate(((w_hbm, w_out), (s_hbm, s_out), (y_hbm, y_out)))
     ]
     bigs = [
         pltpu.make_async_copy(
-            x_hbm.at[:, pl.ds(c * step, step)], x_out.at[:, pl.ds(c * step, step)], x_sem.at[c]
+            x_hbm.at[:, pl.ds(c * step, step)], x_out.at[:, pl.ds(c * step, step)], sem.at[3 + c]
         )
-        for c in range(chunks)
+        for c in range(sum(blocks))
     ]
     for copy in smalls + bigs:
         copy.start()
+    live = place_ref[0] >= 0
     for copy in smalls:
         copy.wait()
-    for c in range(chunks):
-        cut = pl.ds(c * step, step)
-        both = jnp.concatenate([s_out[:, cut], y_out[:, cut]], axis=0)
-        for k, part in enumerate(pieces(both)):
-            z_buf[2 * HIST * k : 2 * HIST * (k + 1), cut] = part
-        w_parts = pieces(w_out[:, cut])
-        place = lax.broadcasted_iota(jnp.int32, (HIST, step), 0)
-        w_rows = jnp.zeros((HIST, step), jnp.float32)
-        for k, part in enumerate(w_parts):
-            w_rows = jnp.where(place == k, part.astype(jnp.float32), w_rows)
-        z_buf[6 * HIST :, cut] = w_rows.astype(jnp.bfloat16)
-    with_x = jnp.zeros((7 * HIST, rows), jnp.float32)
-    with_z = jnp.zeros((7 * HIST, 7 * HIST), jnp.float32)
-    for c in range(chunks):
-        cut = pl.ds(c * step, step)
-        z_part = z_buf[:, cut]
-        with_z = with_z + contract_last(z_part, z_part)
-    for c in range(chunks):
-        cut = pl.ds(c * step, step)
-        z_part = z_buf[:, cut]
-        bigs[c].wait()
-        with_x = with_x + contract_last(z_part, x_out[:, cut])
-    both = 2 * HIST
-    pay[:both, :] = with_x[:both] + (with_x[both : 2 * both] + with_x[2 * both : 3 * both])
-    pay[both:, :] = jnp.zeros((TAIL, rows), jnp.float32)
-    pay[both : both + 1, :] = with_x[3 * both : 3 * both + 1]
-    gram = with_z[:both] + (with_z[both : 2 * both] + with_z[2 * both : 3 * both])
-    of_y = gram[:, HIST:both] + (gram[:, 3 * HIST : 4 * HIST] + gram[:, 5 * HIST : 6 * HIST])
-    at = 6 * HIST
-    of_w = gram[:, at : at + 1] + (gram[:, at + 1 : at + 2] + gram[:, at + 2 : at + 3])
-    wide = jnp.concatenate([of_y[:HIST], of_y[HIST:], of_w[:HIST], of_w[HIST:]], axis=1)
-    for k in range(4):
-        pay[both + 4 : both + 8, LANES * k : LANES * k + both + 2] = wide[4 * k : 4 * k + 4]
+
+    @pl.when(live)
+    def _():
+        part_width = width // 8
+        for c in range(8):
+            cut = pl.ds(c * part_width, part_width)
+            hist = jnp.concatenate([s_out[:, cut], y_out[:, cut]], axis=0)
+            for k, part in enumerate(pieces(hist)):
+                z_buf[both * k : both * (k + 1), cut] = part
+            place = lax.broadcasted_iota(jnp.int32, (both, part_width), 0)
+            w_rows = jnp.zeros((both, part_width), jnp.float32)
+            for k, part in enumerate(pieces(w_out[:, cut])):
+                w_rows = jnp.where(place == k, part.astype(jnp.float32), w_rows)
+            z_buf[3 * both :, cut] = w_rows.astype(jnp.bfloat16)
+        acc[rows:] = contract_last(z_buf[...], z_buf[...])
+
+    at = 0
+    for n, size in enumerate(blocks):
+        for c in range(at, at + size):
+            bigs[c].wait()
+
+        @pl.when(live)
+        def _(n=n, size=size, at=at):
+            cut = pl.ds(at * step, size * step)
+            product = contract_last(x_out[:, cut], z_buf[:, cut])
+            if n == 0:
+                acc[:rows] = product
+            else:
+                acc[:rows] += product
+
+        at += size
+
+    @pl.when(live)
+    def _():
+        with_x = jnp.transpose(acc[:rows])
+        pay[:both] = with_x[:both] + (with_x[both : 2 * both] + with_x[2 * both : 3 * both])
+        pay[both:] = with_x[3 * both : 3 * both + TAIL]
+        with_z = acc[rows:]
+        gram = with_z[:both] + (with_z[both : 2 * both] + with_z[2 * both : 3 * both])
+        of_y = gram[:, HIST:both] + (gram[:, 3 * HIST : 4 * HIST] + gram[:, 5 * HIST : 6 * HIST])
+        at = 6 * HIST
+        of_w = gram[:, at : at + 1] + (gram[:, at + 1 : at + 2] + gram[:, at + 2 : at + 3])
+        wide = jnp.concatenate([of_y[:HIST], of_y[HIST:], of_w[:HIST], of_w[HIST:]], axis=1)
+        for k in range(4):
+            pay[both + 4 : both + 8, LANES * k : LANES * k + both + 2] = wide[4 * k : 4 * k + 4]
 
 
 def second_kernel(chunks, x_ref, own, got, label_ref, pay, gram):
@@ -190,26 +204,30 @@
     both = 2 * HIST
     f32 = jnp.float32
     chunks = 8
+    blocks = (3, 4, 5, 4)
     w_row = weights.reshape(1, width)
-    x_in, w_in, s_in, y_in, pay = pl.pallas_call(
-        lambda *refs: first_kernel(chunks, *refs),
-        in_specs=[ANY] * 4,
+    pay, x_in, w_in, s_in, y_in = pl.pallas_call(
+        lambda *refs: first_kernel(blocks, *refs),
+        in_specs=[SM] + [HBM] * 4,
         out_specs=[VM] * 5,
         out_shape=[
+            pltpu.VMEM((both + TAIL, rows), f32),
             pltpu.VMEM((rows, width), jnp.bfloat16),
             pltpu.VMEM((1, width), f32),
             pltpu.VMEM((HIST, width), f32),
             pltpu.VMEM((HIST, width), f32),
-            pltpu.VMEM((both + TAIL, rows), f32),
         ],
         scratch_shapes=[
-            pltpu.VMEM((7 * HIST, width), jnp.bfloat16),
-            pltpu.SemaphoreType.DMA((3,)),
-            pltpu.SemaphoreType.DMA((chunks,)),
+            pltpu.VMEM((rows + LANES, LANES), f32),
+            pltpu.VMEM((LANES, width), jnp.bfloat16),
+            pltpu.SemaphoreType.DMA((3 + sum(blocks),)),
         ],
         compiler_params=SMALL_GRANT,
         name="load_and_project",
-    )(samples, w_row, hist_s, hist_y)
+    )(
+        lax.axis_index("rows").reshape(1),
+        *(pltpu.with_memory_space_constraint(v, pltpu.HBM) for v in (samples, w_row, hist_s, hist_y)),
+    )
 
     bit = 1
     cols = lax.axis_size("cols")

time: 38.6 us -> 28.9 us (0.75)
  local copies, waits for them, and re-layouts: 6.22 us -> 0.01 us
  Pallas kernels: 11.1 us -> 7.78 us
    unnamed x10 -> x2, local copies, waits for them, and re-layouts: 6.22 us -> 0.01 us
    pallas_call x1, Pallas kernels: 8.44 us -> 5.13 us  [body(): pl.pallas_call(lambda *refs: first_kernel(blocks, *refs), in_specs=[SM] +...]
where the time goes in v2:
time: 28.9 us; the launch traced here: 28.7 us
  starting transfers between devices  10.2 us (35%)
  waiting for transfers between devices  9.36 us (32%)
  Pallas kernels  7.78 us (27%)
  between operations  1.32 us (5%)
    ppermute x6, starting transfers between devices, hop(): return lax.ppermute(values, axis, [(k, k ^ bit) for k in range(size)])  10.2 us
    ppermute x6, waiting for transfers between devices, hop(): return lax.ppermute(values, axis, [(k, k ^ bit) for k in range(size)])  9.36 us
    pallas_call x1, Pallas kernels, body(): pl.pallas_call(lambda *refs: first_kernel(blocks, *refs), in_specs=[SM] +...  5.13 us
    pallas_call x1, Pallas kernels, body(): pl.pallas_call(lambda *refs: second_kernel(chunks, *refs), in_specs=[VM]...  1.2 us
    pallas_call x1, Pallas kernels, body(): pl.pallas_call(lambda *refs: last_kernel(chunks, len(parts), *refs), in_s...  0.88 us
    pallas_call x1, Pallas kernels, body(): pl.pallas_call(solve_kernel, in_specs=[SM, VM], out_specs=VM, out_shape=p...  0.58 us
  transfers between devices with their start and end apart: 6, of which 5 were waited for; matrix products, arithmetic and copies ran while one was open for 0% of the time, Pallas kernels for 2%

profile of v2, /device:TPU:0, one launch (start us, length us, event | category | flops | bytes accessed | tf_op | source)
XLA Modules:
  0.0 28.7 jit_solution(11513915750826903556)
XLA Ops:
  0.6 0.0 copy-start
  0.6 5.1 %load_and_project.1 = (f32[40,512]{1,0:T(8,128)S(1)}, bf16[512,8192]{1,0:T(8,128)(2,1)S(1)}, f32[1,8192]{1,0:T(1,128)S(1)}, f32[16,8192]{1,0:T(8,128)S(1)}, f32[16,8192]{1,0:T(8,128)S(1)}) custom-call(s32[1]{0:T(128)} %bitcast.refs_0_, bf16[512,8192]{1,0:T(8,128)(2,1)} %refs_1_.1, f32[1,8192]{1,0:T(1,128)} %bitcast.6, f32[16,8192]{1,0:T(8,128)} %refs_3_.1, ...), custom_call_target="tpu_custom_call" | custom-call | tf_op jit(solution)/shard_map/load_and_project/pallas_call | solution.py:209
  5.8 3.1 %collective-permute-start = (f32[40,512]{1,0:T(8,128)S(1)}, f32[40,512]{1,0:T(8,128)S(1)}, u32[]{:S(2)}, u32[]{:S(2)}) collective-permute-start(f32[40,512]{1,0:T(8,128)S(1)} %get-tuple-element.12), channel_id=1, source_target_pairs={{0,1},{1,0},{2,3},{3,2},{4,5},{5,4},{6,7},{7,6},{8,9},{9,8},{10,11... | collective-permute-start | bytes 245768 | tf_op jit(solution)/shard_map/ppermute | solution.py:199
  8.8 2.4 %collective-permute-done = f32[40,512]{1,0:T(8,128)S(1)} collective-permute-done((f32[40,512]{1,0:T(8,128)S(1)}, f32[40,512]{1,0:T(8,128)S(1)}, u32[]{:S(2)}, u32[]{:S(2)}) %collective-permute-start) | collective-permute-done | bytes 81952 | tf_op jit(solution)/shard_map/ppermute | solution.py:199
  11.3 2.1 %collective-permute-start.1 = (f32[40,512]{1,0:T(8,128)S(1)}, f32[40,512]{1,0:T(8,128)S(1)}, u32[]{:S(2)}, u32[]{:S(2)}) collective-permute-start(f32[40,512]{1,0:T(8,128)S(1)} %add.6), channel_id=1, source_target_pairs={{0,2},{1,3},{2,0},{3,1},{4,6},{5,7},{6,4},{7,5},{8,10},{9,11},{10,... | collective-permute-start | bytes 245768 | tf_op jit(solution)/shard_map/ppermute | solution.py:199
  13.4 2.4 %collective-permute-done.1 = f32[40,512]{1,0:T(8,128)S(1)} collective-permute-done((f32[40,512]{1,0:T(8,128)S(1)}, f32[40,512]{1,0:T(8,128)S(1)}, u32[]{:S(2)}, u32[]{:S(2)}) %collective-permute-start.1) | collective-permute-done | bytes 81952 | tf_op jit(solution)/shard_map/ppermute | solution.py:199
  15.9 3.1 %collective-permute-start.2 = (f32[40,512]{1,0:T(8,128)S(1)}, f32[40,512]{1,0:T(8,128)S(1)}, u32[]{:S(2)}, u32[]{:S(2)}) collective-permute-start(f32[40,512]{1,0:T(8,128)S(1)} %add.7.refs_1_), channel_id=1, source_target_pairs={{0,4},{1,5},{2,6},{3,7},{4,0},{5,1},{6,2},{7,3},{8,12},{9,13},{10,... | collective-permute-start | bytes 245768 | tf_op jit(solution)/shard_map/ppermute | solution.py:199
  19.0 2.4 %collective-permute-done.2.refs_2_ = f32[40,512]{1,0:T(8,128)S(1)} collective-permute-done((f32[40,512]{1,0:T(8,128)S(1)}, f32[40,512]{1,0:T(8,128)S(1)}, u32[]{:S(2)}, u32[]{:S(2)}) %collective-permute-start.2) | collective-permute-done | bytes 81952 | tf_op jit(solution)/shard_map/ppermute | solution.py:199
  21.4 0.0 copy-done
  21.4 1.2 %residual_and_gradient.1 = (f32[1,8320]{1,0:T(1,128)S(1)}, f32[8,512]{1,0:T(8,128)S(1)}) custom-call(bf16[512,8192]{1,0:T(8,128)(2,1)S(1)} %get-tuple-element.11.refs_0_, f32[40,512]{1,0:T(8,128)S(1)} %add.7.refs_1_, f32[40,512]{1,0:T(8,128)S(1)} %collective-permute-done.2.refs_2_, s32[1,512]{1,0:T(1,128)S(1)} %bitcast.5), custom_call_target="tpu_custom_call" | custom-call | tf_op jit(solution)/shard_map/residual_and_gradient/pallas_call | solution.py:239
  22.6 0.0 collective-permute-start.3
  22.6 1.9 %collective-permute-start.4 = (f32[1,8320]{1,0:T(1,128)S(1)}, f32[1,8320]{1,0:T(1,128)S(1)}, u32[]{:S(2)}, u32[]{:S(2)}) collective-permute-start(f32[1,8320]{1,0:T(1,128)S(1)} %get-tuple-element.13.refs_0_), channel_id=1, source_target_pairs={{0,16},{8,24},{16,0},{24,8},{1,17},{9,25},{17,1},{25,9},{2,18},{10... | collective-permute-start | bytes 99848 | tf_op jit(solution)/shard_map/ppermute | solution.py:199
  24.5 0.1 collective-permute-start.5
  25.2 0.6 %solve_history.1.refs_4_ = f32[40,128]{1,0:T(8,128)S(1)} custom-call(s32[1]{0:T(128)S(6)} %copy.8.counter, f32[8,512]{1,0:T(8,128)S(1)} %get-tuple-element.14.gram), custom_call_target="tpu_custom_call" | custom-call | tf_op jit(solution)/shard_map/solve_history/pallas_call | solution.py:248
  25.8 0.0 collective-permute-done.3.refs_1_
  25.8 0.8 %collective-permute-done.4.refs_2_ = f32[1,8320]{1,0:T(1,128)S(1)} collective-permute-done((f32[1,8320]{1,0:T(1,128)S(1)}, f32[1,8320]{1,0:T(1,128)S(1)}, u32[]{:S(2)}, u32[]{:S(2)}) %collective-permute-start.4) | collective-permute-done | bytes 33312 | tf_op jit(solution)/shard_map/ppermute | solution.py:199
  26.6 1.3 %collective-permute-done.5.refs_3_ = f32[1,8320]{1,0:T(1,128)S(1)} collective-permute-done((f32[1,8320]{1,0:T(1,128)S(1)}, f32[1,8320]{1,0:T(1,128)S(1)}, u32[]{:S(2)}, u32[]{:S(2)}) %collective-permute-start.5) | collective-permute-done | bytes 33312 | tf_op jit(solution)/shard_map/ppermute | solution.py:199
  27.8 0.9 %direction_and_update.1 = (f32[1,8192]{1,0:T(1,128)}, f32[1,8192]{1,0:T(1,128)}) custom-call(f32[1,8320]{1,0:T(1,128)S(1)} %get-tuple-element.13.refs_0_, f32[1,8320]{1,0:T(1,128)S(1)} %collective-permute-done.3.refs_1_, f32[1,8320]{1,0:T(1,128)S(1)} %collective-permute-done.4.refs_2_, f32[1,8320]{1,0:T(1,128)S(1)} %collective-permute-done.5.refs_3_, ...), custom_call_target="tpu_custom_call" | custom-call | tf_op jit(solution)/shard_map/direction_and_update/pallas_call | solution.py:264
  (2 shorter events, 0.0 us)
Async XLA Ops:
  0.6 20.7 %copy-start = (s32[512]{0:T(512)S(1)}, s32[512]{0:T(512)}, u32[]{:S(2)}) copy-start(s32[512]{0:T(512)} %param.7) | copy-start | bytes 6148
  5.8 5.5 %collective-permute-start = (f32[40,512]{1,0:T(8,128)S(1)}, f32[40,512]{1,0:T(8,128)S(1)}, u32[]{:S(2)}, u32[]{:S(2)}) collective-permute-start(f32[40,512]{1,0:T(8,128)S(1)} %get-tuple-element.12), channel_id=1, source_target_pairs={{0,1},{1,0},{2,3},{3,2},{4,5},{5,4},{6,7},{7,6},{8,9},{9,8},{10,11... | collective-permute-start | bytes 245768 | tf_op jit(solution)/shard_map/ppermute | solution.py:199
  11.3 4.5 %collective-permute-start.1 = (f32[40,512]{1,0:T(8,128)S(1)}, f32[40,512]{1,0:T(8,128)S(1)}, u32[]{:S(2)}, u32[]{:S(2)}) collective-permute-start(f32[40,512]{1,0:T(8,128)S(1)} %add.6), channel_id=1, source_target_pairs={{0,2},{1,3},{2,0},{3,1},{4,6},{5,7},{6,4},{7,5},{8,10},{9,11},{10,... | collective-permute-start | bytes 245768 | tf_op jit(solution)/shard_map/ppermute | solution.py:199
  15.9 5.5 %collective-permute-start.2 = (f32[40,512]{1,0:T(8,128)S(1)}, f32[40,512]{1,0:T(8,128)S(1)}, u32[]{:S(2)}, u32[]{:S(2)}) collective-permute-start(f32[40,512]{1,0:T(8,128)S(1)} %add.7.refs_1_), channel_id=1, source_target_pairs={{0,4},{1,5},{2,6},{3,7},{4,0},{5,1},{6,2},{7,3},{8,12},{9,13},{10,... | collective-permute-start | bytes 245768 | tf_op jit(solution)/shard_map/ppermute | solution.py:199
  22.6 3.2 %collective-permute-start.3 = (f32[1,8320]{1,0:T(1,128)S(1)}, f32[1,8320]{1,0:T(1,128)S(1)}, u32[]{:S(2)}, u32[]{:S(2)}) collective-permute-start(f32[1,8320]{1,0:T(1,128)S(1)} %get-tuple-element.13.refs_0_), channel_id=1, source_target_pairs={{0,8},{8,0},{16,24},{24,16},{1,9},{9,1},{17,25},{25,17},{2,10},{10... | collective-permute-start | bytes 99848 | tf_op jit(solution)/shard_map/ppermute | solution.py:199
  22.6 4.0 %collective-permute-start.4 = (f32[1,8320]{1,0:T(1,128)S(1)}, f32[1,8320]{1,0:T(1,128)S(1)}, u32[]{:S(2)}, u32[]{:S(2)}) collective-permute-start(f32[1,8320]{1,0:T(1,128)S(1)} %get-tuple-element.13.refs_0_), channel_id=1, source_target_pairs={{0,16},{8,24},{16,0},{24,8},{1,17},{9,25},{17,1},{25,9},{2,18},{10... | collective-permute-start | bytes 99848 | tf_op jit(solution)/shard_map/ppermute | solution.py:199
  24.5 3.4 %collective-permute-start.5 = (f32[1,8320]{1,0:T(1,128)S(1)}, f32[1,8320]{1,0:T(1,128)S(1)}, u32[]{:S(2)}, u32[]{:S(2)}) collective-permute-start(f32[1,8320]{1,0:T(1,128)S(1)} %get-tuple-element.13.refs_0_), channel_id=1, source_target_pairs={{0,24},{8,16},{16,8},{24,0},{1,25},{9,17},{17,9},{25,1},{2,26},{10... | collective-permute-start | bytes 99848 | tf_op jit(solution)/shard_map/ppermute | solution.py:199

commit v3 on v2

--- a/solution.py
+++ b/solution.py
@@ -7,7 +7,8 @@
 
 HIST = 16
 LANES = 128
-TAIL = 8
+FOLD = 4
+SPOT = 64
 
 penalty = 4.0
 step_length = 0.5
@@ -87,47 +88,49 @@
     @pl.when(live)
     def _():
         with_x = jnp.transpose(acc[:rows])
-        pay[:both] = with_x[:both] + (with_x[both : 2 * both] + with_x[2 * both : 3 * both])
-        pay[both:] = with_x[3 * both : 3 * both + TAIL]
+        cross = with_x[:both] + (with_x[both : 2 * both] + with_x[2 * both : 3 * both])
+        for k in range(both // FOLD):
+            pay[k] = cross[FOLD * k : FOLD * (k + 1)]
         with_z = acc[rows:]
         gram = with_z[:both] + (with_z[both : 2 * both] + with_z[2 * both : 3 * both])
         of_y = gram[:, HIST:both] + (gram[:, 3 * HIST : 4 * HIST] + gram[:, 5 * HIST : 6 * HIST])
         at = 6 * HIST
         of_w = gram[:, at : at + 1] + (gram[:, at + 1 : at + 2] + gram[:, at + 2 : at + 3])
-        wide = jnp.concatenate([of_y[:HIST], of_y[HIST:], of_w[:HIST], of_w[HIST:]], axis=1)
-        for k in range(4):
-            pay[both + 4 : both + 8, LANES * k : LANES * k + both + 2] = wide[4 * k : 4 * k + 4]
+        blank = jnp.zeros((HIST, SPOT - both - 2), jnp.float32)
+        wide = jnp.concatenate([of_y[:HIST], of_y[HIST:], of_w[:HIST], of_w[HIST:], blank], axis=1)
+        wide = jnp.concatenate([wide, jnp.zeros((2, SPOT), jnp.float32)], axis=0)
+        laid = jnp.concatenate([wide[3 * k : 3 * k + 3] for k in range(6)], axis=1)
+        last = both // FOLD
+        pay[last] = jnp.zeros((FOLD, rows), jnp.float32)
+        pay[last, :1] = with_x[3 * both : 3 * both + 1]
+        pay[last, 1:, : 6 * SPOT] = laid
 
 
 def second_kernel(chunks, x_ref, own, got, label_ref, pay, gram):
     both = 2 * HIST
     rows, width = x_ref.shape
     step = width // chunks
-    tail = own[both:, :] + got[both:, :]
+    last = both // FOLD
+    tail = own[last] + got[last]
     gram[...] = tail
     margin = tail[0:1, :]
     resid = (jax.nn.sigmoid(margin) - label_ref[...].astype(jnp.float32)).astype(jnp.bfloat16)
     for c in range(chunks):
         cut = pl.ds(c * step, step)
         pay[:, cut] = jnp.dot(resid, x_ref[:, cut], preferred_element_type=jnp.float32)
-    cross = (own[:both, :] + got[:both, :]) * resid.astype(jnp.float32)
+    products = jnp.concatenate([own[k] + got[k] for k in range(last)], axis=0)
+    cross = products * resid.astype(jnp.float32)
     column = jnp.sum(cross, axis=1, keepdims=True)
     row_at = lax.broadcasted_iota(jnp.int32, (both, LANES), 0)
     lane_at = lax.broadcasted_iota(jnp.int32, (both, LANES), 1)
     pay[:, width:] = jnp.sum(jnp.where(row_at == lane_at, column, 0.0), axis=0, keepdims=True)
 
 
-def to_column(row, count):
-    row_at = lax.broadcasted_iota(jnp.int32, (count, count), 0)
-    lane_at = lax.broadcasted_iota(jnp.int32, (count, count), 1)
-    return jnp.sum(jnp.where(row_at == lane_at, row, 0.0), axis=1, keepdims=True)
-
-
 def solve_kernel(counter, gram, out):
     newest = lax.rem(counter[0], HIST)
     wide = jnp.concatenate(
-        [gram[4:8, LANES * k : LANES * (k + 1)] for k in range(4)], axis=0
-    )
+        [gram[1:, SPOT * k : SPOT * (k + 1)] for k in range(6)], axis=0
+    )[:HIST]
     sy = wide[:, :HIST]
     yy = wide[:, HIST : 2 * HIST]
     row_at = lax.broadcasted_iota(jnp.int32, (HIST, HIST), 0)
@@ -211,7 +214,7 @@
         in_specs=[SM] + [HBM] * 4,
         out_specs=[VM] * 5,
         out_shape=[
-            pltpu.VMEM((both + TAIL, rows), f32),
+            pltpu.VMEM((both // FOLD + 1, FOLD, rows), f32),
             pltpu.VMEM((rows, width), jnp.bfloat16),
             pltpu.VMEM((1, width), f32),
             pltpu.VMEM((HIST, width), f32),
@@ -240,7 +243,7 @@
         lambda *refs: second_kernel(chunks, *refs),
         in_specs=[VM] * 4,
         out_specs=[VM] * 2,
-        out_shape=[pltpu.VMEM((1, width + LANES), f32), pltpu.VMEM((TAIL, rows), f32)],
+        out_shape=[pltpu.VMEM((1, width + LANES), f32), pltpu.VMEM((FOLD, rows), f32)],
         compiler_params=SMALL_GRANT,
         name="residual_and_gradient",
     )(x_in, pay, got, labels.reshape(1, rows))
@@ -249,7 +252,7 @@
         solve_kernel,
         in_specs=[SM, VM],
         out_specs=VM,
-        out_shape=pltpu.VMEM((both + TAIL, LANES), f32),
+        out_shape=pltpu.VMEM((both + 8, LANES), f32),
         compiler_params=SMALL_GRANT,
         name="solve_history",
     )(counter, gram)

time: 28.9 us -> 28.6 us (0.990)
  waiting for transfers between devices: 9.36 us -> 9 us
    ppermute x6, waiting for transfers between devices: 9.36 us -> 9 us  [hop(): return lax.ppermute(values, axis, [(k, k ^ bit) for k in range(size)])]
where the time goes in v3:
time: 28.6 us; the launch traced here: 28.5 us
  starting transfers between devices  10.3 us (36%)
  waiting for transfers between devices  9 us (31%)
  Pallas kernels  7.84 us (27%)
  between operations  1.32 us (5%)
    ppermute x6, starting transfers between devices, hop(): return lax.ppermute(values, axis, [(k, k ^ bit) for k in range(size)])  10.3 us
    ppermute x6, waiting for transfers between devices, hop(): return lax.ppermute(values, axis, [(k, k ^ bit) for k in range(size)])  9 us
    pallas_call x1, Pallas kernels, body(): pl.pallas_call(lambda *refs: first_kernel(blocks, *refs), in_specs=[SM] +...  5.1 us
    pallas_call x1, Pallas kernels, body(): pl.pallas_call(lambda *refs: second_kernel(chunks, *refs), in_specs=[VM]...  1.21 us
    pallas_call x1, Pallas kernels, body(): pl.pallas_call(lambda *refs: last_kernel(chunks, len(parts), *refs), in_s...  0.88 us
    pallas_call x1, Pallas kernels, body(): pl.pallas_call(solve_kernel, in_specs=[SM, VM], out_specs=VM, out_shape=p...  0.65 us
  transfers between devices with their start and end apart: 6, of which 5 were waited for; matrix products, arithmetic and copies ran while one was open for 0% of the time, Pallas kernels for 2%

profile of v3, /device:TPU:0, one launch (start us, length us, event | category | flops | bytes accessed | tf_op | source)
XLA Modules:
  0.0 28.5 jit_solution(1893583957608993991)
XLA Ops:
  0.6 0.0 copy-start
  0.6 5.1 %load_and_project.1 = (f32[9,4,512]{2,1,0:T(4,128)S(1)}, bf16[512,8192]{1,0:T(8,128)(2,1)S(1)}, f32[1,8192]{1,0:T(1,128)S(1)}, f32[16,8192]{1,0:T(8,128)S(1)}, f32[16,8192]{1,0:T(8,128)S(1)}) custom-call(s32[1]{0:T(128)} %bitcast.refs_0_, bf16[512,8192]{1,0:T(8,128)(2,1)} %refs_1_.1, f32[1,8192]{1,0:T(1,128)} %bitcast.6, f32[16,8192]{1,0:T(8,128)} %refs_3_.1, ...), custom_call_target="tpu_custom_call" | custom-call | tf_op jit(solution)/shard_map/load_and_project/pallas_call | solution.py:212
  5.8 3.1 %collective-permute-start = (f32[9,4,512]{2,1,0:T(4,128)S(1)}, f32[9,4,512]{2,1,0:T(4,128)S(1)}, u32[]{:S(2)}, u32[]{:S(2)}) collective-permute-start(f32[9,4,512]{2,1,0:T(4,128)S(1)} %get-tuple-element.12), channel_id=1, source_target_pairs={{0,1},{1,0},{2,3},{3,2},{4,5},{5,4},{6,7},{7,6},{8,9},{9,8},{10,11... | collective-permute-start | bytes 221192 | tf_op jit(solution)/shard_map/ppermute | solution.py:202
  8.8 2.3 %collective-permute-done = f32[9,4,512]{2,1,0:T(4,128)S(1)} collective-permute-done((f32[9,4,512]{2,1,0:T(4,128)S(1)}, f32[9,4,512]{2,1,0:T(4,128)S(1)}, u32[]{:S(2)}, u32[]{:S(2)}) %collective-permute-start) | collective-permute-done | bytes 73760 | tf_op jit(solution)/shard_map/ppermute | solution.py:202
  11.2 2.1 %collective-permute-start.1 = (f32[9,4,512]{2,1,0:T(4,128)S(1)}, f32[9,4,512]{2,1,0:T(4,128)S(1)}, u32[]{:S(2)}, u32[]{:S(2)}) collective-permute-start(f32[9,4,512]{2,1,0:T(4,128)S(1)} %add.6), channel_id=1, source_target_pairs={{0,2},{1,3},{2,0},{3,1},{4,6},{5,7},{6,4},{7,5},{8,10},{9,11},{10,... | collective-permute-start | bytes 221192 | tf_op jit(solution)/shard_map/ppermute | solution.py:202
  13.3 2.3 %collective-permute-done.1 = f32[9,4,512]{2,1,0:T(4,128)S(1)} collective-permute-done((f32[9,4,512]{2,1,0:T(4,128)S(1)}, f32[9,4,512]{2,1,0:T(4,128)S(1)}, u32[]{:S(2)}, u32[]{:S(2)}) %collective-permute-start.1) | collective-permute-done | bytes 73760 | tf_op jit(solution)/shard_map/ppermute | solution.py:202
  15.7 3.1 %collective-permute-start.2 = (f32[9,4,512]{2,1,0:T(4,128)S(1)}, f32[9,4,512]{2,1,0:T(4,128)S(1)}, u32[]{:S(2)}, u32[]{:S(2)}) collective-permute-start(f32[9,4,512]{2,1,0:T(4,128)S(1)} %add.7.refs_1_), channel_id=1, source_target_pairs={{0,4},{1,5},{2,6},{3,7},{4,0},{5,1},{6,2},{7,3},{8,12},{9,13},{10,... | collective-permute-start | bytes 221192 | tf_op jit(solution)/shard_map/ppermute | solution.py:202
  18.8 2.3 %collective-permute-done.2.refs_2_ = f32[9,4,512]{2,1,0:T(4,128)S(1)} collective-permute-done((f32[9,4,512]{2,1,0:T(4,128)S(1)}, f32[9,4,512]{2,1,0:T(4,128)S(1)}, u32[]{:S(2)}, u32[]{:S(2)}) %collective-permute-start.2) | collective-permute-done | bytes 73760 | tf_op jit(solution)/shard_map/ppermute | solution.py:202
  21.1 0.0 copy-done
  21.1 1.2 %residual_and_gradient.1 = (f32[1,8320]{1,0:T(1,128)S(1)}, f32[4,512]{1,0:T(4,128)S(1)}) custom-call(bf16[512,8192]{1,0:T(8,128)(2,1)S(1)} %get-tuple-element.11.refs_0_, f32[9,4,512]{2,1,0:T(4,128)S(1)} %add.7.refs_1_, f32[9,4,512]{2,1,0:T(4,128)S(1)} %collective-permute-done.2.refs_2_, s32[1,512]{1,0:T(1,128)S(1)} %bitcast.5), custom_call_target="tpu_custom_call" | custom-call | tf_op jit(solution)/shard_map/residual_and_gradient/pallas_call | solution.py:242
  22.3 0.0 collective-permute-start.3
  22.3 1.9 %collective-permute-start.4 = (f32[1,8320]{1,0:T(1,128)S(1)}, f32[1,8320]{1,0:T(1,128)S(1)}, u32[]{:S(2)}, u32[]{:S(2)}) collective-permute-start(f32[1,8320]{1,0:T(1,128)S(1)} %get-tuple-element.13.refs_0_), channel_id=1, source_target_pairs={{0,16},{8,24},{16,0},{24,8},{1,17},{9,25},{17,1},{25,9},{2,18},{10... | collective-permute-start | bytes 99848 | tf_op jit(solution)/shard_map/ppermute | solution.py:202
  24.2 0.0 collective-permute-start.5
  24.9 0.7 %solve_history.1.refs_4_ = f32[40,128]{1,0:T(8,128)S(1)} custom-call(s32[1]{0:T(128)S(6)} %copy.8.counter, f32[4,512]{1,0:T(4,128)S(1)} %get-tuple-element.14.gram), custom_call_target="tpu_custom_call" | custom-call | tf_op jit(solution)/shard_map/solve_history/pallas_call | solution.py:251
  25.6 0.0 collective-permute-done.3.refs_1_
  25.6 0.7 %collective-permute-done.4.refs_2_ = f32[1,8320]{1,0:T(1,128)S(1)} collective-permute-done((f32[1,8320]{1,0:T(1,128)S(1)}, f32[1,8320]{1,0:T(1,128)S(1)}, u32[]{:S(2)}, u32[]{:S(2)}) %collective-permute-start.4) | collective-permute-done | bytes 33312 | tf_op jit(solution)/shard_map/ppermute | solution.py:202
  26.3 1.3 %collective-permute-done.5.refs_3_ = f32[1,8320]{1,0:T(1,128)S(1)} collective-permute-done((f32[1,8320]{1,0:T(1,128)S(1)}, f32[1,8320]{1,0:T(1,128)S(1)}, u32[]{:S(2)}, u32[]{:S(2)}) %collective-permute-start.5) | collective-permute-done | bytes 33312 | tf_op jit(solution)/shard_map/ppermute | solution.py:202
  27.6 0.9 %direction_and_update.1 = (f32[1,8192]{1,0:T(1,128)}, f32[1,8192]{1,0:T(1,128)}) custom-call(f32[1,8320]{1,0:T(1,128)S(1)} %get-tuple-element.13.refs_0_, f32[1,8320]{1,0:T(1,128)S(1)} %collective-permute-done.3.refs_1_, f32[1,8320]{1,0:T(1,128)S(1)} %collective-permute-done.4.refs_2_, f32[1,8320]{1,0:T(1,128)S(1)} %collective-permute-done.5.refs_3_, ...), custom_call_target="tpu_custom_call" | custom-call | tf_op jit(solution)/shard_map/direction_and_update/pallas_call | solution.py:267
  (2 shorter events, 0.0 us)
Async XLA Ops:
  0.6 20.5 %copy-start = (s32[512]{0:T(512)S(1)}, s32[512]{0:T(512)}, u32[]{:S(2)}) copy-start(s32[512]{0:T(512)} %param.7) | copy-start | bytes 6148
  5.8 5.4 %collective-permute-start = (f32[9,4,512]{2,1,0:T(4,128)S(1)}, f32[9,4,512]{2,1,0:T(4,128)S(1)}, u32[]{:S(2)}, u32[]{:S(2)}) collective-permute-start(f32[9,4,512]{2,1,0:T(4,128)S(1)} %get-tuple-element.12), channel_id=1, source_target_pairs={{0,1},{1,0},{2,3},{3,2},{4,5},{5,4},{6,7},{7,6},{8,9},{9,8},{10,11... | collective-permute-start | bytes 221192 | tf_op jit(solution)/shard_map/ppermute | solution.py:202
  11.2 4.5 %collective-permute-start.1 = (f32[9,4,512]{2,1,0:T(4,128)S(1)}, f32[9,4,512]{2,1,0:T(4,128)S(1)}, u32[]{:S(2)}, u32[]{:S(2)}) collective-permute-start(f32[9,4,512]{2,1,0:T(4,128)S(1)} %add.6), channel_id=1, source_target_pairs={{0,2},{1,3},{2,0},{3,1},{4,6},{5,7},{6,4},{7,5},{8,10},{9,11},{10,... | collective-permute-start | bytes 221192 | tf_op jit(solution)/shard_map/ppermute | solution.py:202
  15.7 5.4 %collective-permute-start.2 = (f32[9,4,512]{2,1,0:T(4,128)S(1)}, f32[9,4,512]{2,1,0:T(4,128)S(1)}, u32[]{:S(2)}, u32[]{:S(2)}) collective-permute-start(f32[9,4,512]{2,1,0:T(4,128)S(1)} %add.7.refs_1_), channel_id=1, source_target_pairs={{0,4},{1,5},{2,6},{3,7},{4,0},{5,1},{6,2},{7,3},{8,12},{9,13},{10,... | collective-permute-start | bytes 221192 | tf_op jit(solution)/shard_map/ppermute | solution.py:202
  22.3 3.3 %collective-permute-start.3 = (f32[1,8320]{1,0:T(1,128)S(1)}, f32[1,8320]{1,0:T(1,128)S(1)}, u32[]{:S(2)}, u32[]{:S(2)}) collective-permute-start(f32[1,8320]{1,0:T(1,128)S(1)} %get-tuple-element.13.refs_0_), channel_id=1, source_target_pairs={{0,8},{8,0},{16,24},{24,16},{1,9},{9,1},{17,25},{25,17},{2,10},{10... | collective-permute-start | bytes 99848 | tf_op jit(solution)/shard_map/ppermute | solution.py:202
  22.3 4.0 %collective-permute-start.4 = (f32[1,8320]{1,0:T(1,128)S(1)}, f32[1,8320]{1,0:T(1,128)S(1)}, u32[]{:S(2)}, u32[]{:S(2)}) collective-permute-start(f32[1,8320]{1,0:T(1,128)S(1)} %get-tuple-element.13.refs_0_), channel_id=1, source_target_pairs={{0,16},{8,24},{16,0},{24,8},{1,17},{9,25},{17,1},{25,9},{2,18},{10... | collective-permute-start | bytes 99848 | tf_op jit(solution)/shard_map/ppermute | solution.py:202
  24.2 3.4 %collective-permute-start.5 = (f32[1,8320]{1,0:T(1,128)S(1)}, f32[1,8320]{1,0:T(1,128)S(1)}, u32[]{:S(2)}, u32[]{:S(2)}) collective-permute-start(f32[1,8320]{1,0:T(1,128)S(1)} %get-tuple-element.13.refs_0_), channel_id=1, source_target_pairs={{0,24},{8,16},{16,8},{24,0},{1,25},{9,17},{17,9},{25,1},{2,26},{10... | collective-permute-start | bytes 99848 | tf_op jit(solution)/shard_map/ppermute | solution.py:202

commit v4 on v3

--- a/solution.py
+++ b/solution.py
@@ -4,6 +4,7 @@
 from jax.experimental import pallas as pl
 from jax.experimental.pallas import tpu as pltpu
 from jax.sharding import PartitionSpec as P
+
 
 HIST = 16
 LANES = 128
@@ -108,7 +109,7 @@
 
 def second_kernel(chunks, x_ref, own, got, label_ref, pay, gram):
     both = 2 * HIST
-    rows, width = x_ref.shape
+    _, width = x_ref.shape
     step = width // chunks
     last = both // FOLD
     tail = own[last] + got[last]
@@ -232,12 +233,16 @@
         *(pltpu.with_memory_space_constraint(v, pltpu.HBM) for v in (samples, w_row, hist_s, hist_y)),
     )
 
-    bit = 1
     cols = lax.axis_size("cols")
-    while 2 * bit < cols:
+    bit = cols // 2
+    while bit > 2:
         pay = pay + hop(pay, "cols", bit)
-        bit *= 2
-    got = hop(pay, "cols", bit) if cols > 1 else jnp.zeros_like(pay)
+        bit //= 2
+    near = {k: hop(pay, "cols", k) for k in (1, 2, 3) if k < cols}
+    if cols >= 4:
+        own, got = pay + near[1], near[2] + near[3]
+    else:
+        own, got = pay, near[1] if cols > 1 else jnp.zeros_like(pay)
 
     part, gram = pl.pallas_call(
         lambda *refs: second_kernel(chunks, *refs),
@@ -246,7 +251,7 @@
         out_shape=[pltpu.VMEM((1, width + LANES), f32), pltpu.VMEM((FOLD, rows), f32)],
         compiler_params=SMALL_GRANT,
         name="residual_and_gradient",
-    )(x_in, pay, got, labels.reshape(1, rows))
+    )(x_in, own, got, labels.reshape(1, rows))
 
     coefs = pl.pallas_call(
         solve_kernel,
@@ -278,4 +283,5 @@
 def solution(mesh):
     in_specs = (P("rows", "cols"), P("rows"), P("cols"), P(None, "cols"), P(None, "cols"), P())
     out_specs = (P("cols"), P("cols"))
+
     return jax.shard_map(body, mesh=mesh, in_specs=in_specs, out_specs=out_specs, check_vma=False)

time: 28.6 us -> 28.5 us (level)
  starting transfers between devices: 10.3 us -> 9.55 us
  waiting for transfers between devices: 9 us -> 9.58 us
    ppermute x6 -> x7, starting transfers between devices: 10.3 us -> 9.55 us  [hop(): return lax.ppermute(values, axis, [(k, k ^ bit) for k in range(size)])]
    ppermute x6 -> x7, waiting for transfers between devices: 9 us -> 9.58 us  [hop(): return lax.ppermute(values, axis, [(k, k ^ bit) for k in range(size)])]
  transfers between devices with their start and end apart: 6 -> 7, of which waited for: 5 -> 6; matrix products, arithmetic and copies ran while one was open for 0% -> 0% of each run, Pallas kernels for 2% -> 2%
where the time goes in v4:
time: 28.5 us; the launch traced here: 28.4 us
  waiting for transfers between devices  9.58 us (34%)
  starting transfers between devices  9.55 us (34%)
  Pallas kernels  7.84 us (28%)
  between operations  1.33 us (5%)
    ppermute x7, waiting for transfers between devices, hop(): return lax.ppermute(values, axis, [(k, k ^ bit) for k in range(size)])  9.58 us
    ppermute x7, starting transfers between devices, hop(): return lax.ppermute(values, axis, [(k, k ^ bit) for k in range(size)])  9.55 us
    pallas_call x1, Pallas kernels, body(): pl.pallas_call(lambda *refs: first_kernel(blocks, *refs), in_specs=[SM] +...  5.1 us
    pallas_call x1, Pallas kernels, body(): pl.pallas_call(lambda *refs: second_kernel(chunks, *refs), in_specs=[VM]...  1.21 us
    pallas_call x1, Pallas kernels, body(): pl.pallas_call(lambda *refs: last_kernel(chunks, len(parts), *refs), in_s...  0.88 us
    pallas_call x1, Pallas kernels, body(): pl.pallas_call(solve_kernel, in_specs=[SM, VM], out_specs=VM, out_shape=p...  0.65 us
  transfers between devices with their start and end apart: 7, of which 6 were waited for; matrix products, arithmetic and copies ran while one was open for 0% of the time, Pallas kernels for 2%

profile of v4, /device:TPU:0, one launch (start us, length us, event | category | flops | bytes accessed | tf_op | source)
XLA Modules:
  0.0 28.4 jit_solution(11657887843461882502)
XLA Ops:
  0.6 0.0 copy-start
  0.6 5.1 %load_and_project.1 = (f32[9,4,512]{2,1,0:T(4,128)S(1)}, bf16[512,8192]{1,0:T(8,128)(2,1)S(1)}, f32[1,8192]{1,0:T(1,128)S(1)}, f32[16,8192]{1,0:T(8,128)S(1)}, f32[16,8192]{1,0:T(8,128)S(1)}) custom-call(s32[1]{0:T(128)} %bitcast.refs_0_, bf16[512,8192]{1,0:T(8,128)(2,1)} %refs_1_.1, f32[1,8192]{1,0:T(1,128)} %bitcast.6, f32[16,8192]{1,0:T(8,128)} %refs_3_.1, ...), custom_call_target="tpu_custom_call" | custom-call | tf_op jit(solution)/shard_map/load_and_project/pallas_call | solution.py:213
  5.8 4.1 %collective-permute-start = (f32[9,4,512]{2,1,0:T(4,128)S(1)}, f32[9,4,512]{2,1,0:T(4,128)S(1)}, u32[]{:S(2)}, u32[]{:S(2)}) collective-permute-start(f32[9,4,512]{2,1,0:T(4,128)S(1)} %get-tuple-element.12), channel_id=1, source_target_pairs={{0,4},{1,5},{2,6},{3,7},{4,0},{5,1},{6,2},{7,3},{8,12},{9,13},{10,... | collective-permute-start | bytes 221192 | tf_op jit(solution)/shard_map/ppermute | solution.py:203
  9.9 3.9 %collective-permute-done = f32[9,4,512]{2,1,0:T(4,128)S(1)} collective-permute-done((f32[9,4,512]{2,1,0:T(4,128)S(1)}, f32[9,4,512]{2,1,0:T(4,128)S(1)}, u32[]{:S(2)}, u32[]{:S(2)}) %collective-permute-start) | collective-permute-done | bytes 73760 | tf_op jit(solution)/shard_map/ppermute | solution.py:203
  13.8 1.8 %collective-permute-start.1 = (f32[9,4,512]{2,1,0:T(4,128)S(1)}, f32[9,4,512]{2,1,0:T(4,128)S(1)}, u32[]{:S(2)}, u32[]{:S(2)}) collective-permute-start(f32[9,4,512]{2,1,0:T(4,128)S(1)} %add.9), channel_id=1, source_target_pairs={{0,1},{1,0},{2,3},{3,2},{4,5},{5,4},{6,7},{7,6},{8,9},{9,8},{10,11... | collective-permute-start | bytes 221192 | tf_op jit(solution)/shard_map/ppermute | solution.py:203
  15.6 0.5 %collective-permute-start.2 = (f32[9,4,512]{2,1,0:T(4,128)S(1)}, f32[9,4,512]{2,1,0:T(4,128)S(1)}, u32[]{:S(2)}, u32[]{:S(2)}) collective-permute-start(f32[9,4,512]{2,1,0:T(4,128)S(1)} %add.9), channel_id=1, source_target_pairs={{0,2},{1,3},{2,0},{3,1},{4,6},{5,7},{6,4},{7,5},{8,10},{9,11},{10,... | collective-permute-start | bytes 221192 | tf_op jit(solution)/shard_map/ppermute | solution.py:203
  16.1 1.3 %collective-permute-start.3 = (f32[9,4,512]{2,1,0:T(4,128)S(1)}, f32[9,4,512]{2,1,0:T(4,128)S(1)}, u32[]{:S(2)}, u32[]{:S(2)}) collective-permute-start(f32[9,4,512]{2,1,0:T(4,128)S(1)} %add.9), channel_id=1, source_target_pairs={{0,3},{1,2},{2,1},{3,0},{4,7},{5,6},{6,5},{7,4},{8,11},{9,10},{10,... | collective-permute-start | bytes 221192 | tf_op jit(solution)/shard_map/ppermute | solution.py:203
  17.4 0.9 %collective-permute-done.1 = f32[9,4,512]{2,1,0:T(4,128)S(1)} collective-permute-done((f32[9,4,512]{2,1,0:T(4,128)S(1)}, f32[9,4,512]{2,1,0:T(4,128)S(1)}, u32[]{:S(2)}, u32[]{:S(2)}) %collective-permute-start.1) | collective-permute-done | bytes 73760 | tf_op jit(solution)/shard_map/ppermute | solution.py:203
  18.3 1.6 %collective-permute-done.2 = f32[9,4,512]{2,1,0:T(4,128)S(1)} collective-permute-done((f32[9,4,512]{2,1,0:T(4,128)S(1)}, f32[9,4,512]{2,1,0:T(4,128)S(1)}, u32[]{:S(2)}, u32[]{:S(2)}) %collective-permute-start.2) | collective-permute-done | bytes 73760 | tf_op jit(solution)/shard_map/ppermute | solution.py:203
  20.0 1.4 %collective-permute-done.3 = f32[9,4,512]{2,1,0:T(4,128)S(1)} collective-permute-done((f32[9,4,512]{2,1,0:T(4,128)S(1)}, f32[9,4,512]{2,1,0:T(4,128)S(1)}, u32[]{:S(2)}, u32[]{:S(2)}) %collective-permute-start.3) | collective-permute-done | bytes 73760 | tf_op jit(solution)/shard_map/ppermute | solution.py:203
  21.4 0.0 copy-done
  21.4 1.2 %residual_and_gradient.1 = (f32[1,8320]{1,0:T(1,128)S(1)}, f32[4,512]{1,0:T(4,128)S(1)}) custom-call(bf16[512,8192]{1,0:T(8,128)(2,1)S(1)} %get-tuple-element.11.refs_0_, f32[9,4,512]{2,1,0:T(4,128)S(1)} %add.10.refs_1_, f32[9,4,512]{2,1,0:T(4,128)S(1)} %add.11.refs_2_, s32[1,512]{1,0:T(1,128)S(1)} %bitcast.5), custom_call_target="tpu_custom_call" | custom-call | tf_op jit(solution)/shard_map/residual_and_gradient/pallas_call | solution.py:247
  22.6 0.0 collective-permute-start.4
  22.6 1.6 %collective-permute-start.5 = (f32[1,8320]{1,0:T(1,128)S(1)}, f32[1,8320]{1,0:T(1,128)S(1)}, u32[]{:S(2)}, u32[]{:S(2)}) collective-permute-start(f32[1,8320]{1,0:T(1,128)S(1)} %get-tuple-element.13.refs_0_), channel_id=1, source_target_pairs={{0,16},{8,24},{16,0},{24,8},{1,17},{9,25},{17,1},{25,9},{2,18},{10... | collective-permute-start | bytes 99848 | tf_op jit(solution)/shard_map/ppermute | solution.py:203
  24.1 0.3 %collective-permute-start.6 = (f32[1,8320]{1,0:T(1,128)S(1)}, f32[1,8320]{1,0:T(1,128)S(1)}, u32[]{:S(2)}, u32[]{:S(2)}) collective-permute-start(f32[1,8320]{1,0:T(1,128)S(1)} %get-tuple-element.13.refs_0_), channel_id=1, source_target_pairs={{0,24},{8,16},{16,8},{24,0},{1,25},{9,17},{17,9},{25,1},{2,26},{10... | collective-permute-start | bytes 99848 | tf_op jit(solution)/shard_map/ppermute | solution.py:203
  25.1 0.7 %solve_history.1.refs_4_ = f32[40,128]{1,0:T(8,128)S(1)} custom-call(s32[1]{0:T(128)S(6)} %copy.8.counter, f32[4,512]{1,0:T(4,128)S(1)} %get-tuple-element.14.gram), custom_call_target="tpu_custom_call" | custom-call | tf_op jit(solution)/shard_map/solve_history/pallas_call | solution.py:256
  25.7 0.0 collective-permute-done.4.refs_1_
  25.7 0.8 %collective-permute-done.5.refs_2_ = f32[1,8320]{1,0:T(1,128)S(1)} collective-permute-done((f32[1,8320]{1,0:T(1,128)S(1)}, f32[1,8320]{1,0:T(1,128)S(1)}, u32[]{:S(2)}, u32[]{:S(2)}) %collective-permute-start.5) | collective-permute-done | bytes 33312 | tf_op jit(solution)/shard_map/ppermute | solution.py:203
  26.6 0.9 %collective-permute-done.6.refs_3_ = f32[1,8320]{1,0:T(1,128)S(1)} collective-permute-done((f32[1,8320]{1,0:T(1,128)S(1)}, f32[1,8320]{1,0:T(1,128)S(1)}, u32[]{:S(2)}, u32[]{:S(2)}) %collective-permute-start.6) | collective-permute-done | bytes 33312 | tf_op jit(solution)/shard_map/ppermute | solution.py:203
  27.5 0.9 %direction_and_update.1 = (f32[1,8192]{1,0:T(1,128)}, f32[1,8192]{1,0:T(1,128)}) custom-call(f32[1,8320]{1,0:T(1,128)S(1)} %get-tuple-element.13.refs_0_, f32[1,8320]{1,0:T(1,128)S(1)} %collective-permute-done.4.refs_1_, f32[1,8320]{1,0:T(1,128)S(1)} %collective-permute-done.5.refs_2_, f32[1,8320]{1,0:T(1,128)S(1)} %collective-permute-done.6.refs_3_, ...), custom_call_target="tpu_custom_call" | custom-call | tf_op jit(solution)/shard_map/direction_and_update/pallas_call | solution.py:272
  (3 shorter events, 0.1 us)
Async XLA Ops:
  0.6 20.7 %copy-start = (s32[512]{0:T(512)S(1)}, s32[512]{0:T(512)}, u32[]{:S(2)}) copy-start(s32[512]{0:T(512)} %param.7) | copy-start | bytes 6148
  5.8 8.0 %collective-permute-start = (f32[9,4,512]{2,1,0:T(4,128)S(1)}, f32[9,4,512]{2,1,0:T(4,128)S(1)}, u32[]{:S(2)}, u32[]{:S(2)}) collective-permute-start(f32[9,4,512]{2,1,0:T(4,128)S(1)} %get-tuple-element.12), channel_id=1, source_target_pairs={{0,4},{1,5},{2,6},{3,7},{4,0},{5,1},{6,2},{7,3},{8,12},{9,13},{10,... | collective-permute-start | bytes 221192 | tf_op jit(solution)/shard_map/ppermute | solution.py:203
  13.8 4.5 %collective-permute-start.1 = (f32[9,4,512]{2,1,0:T(4,128)S(1)}, f32[9,4,512]{2,1,0:T(4,128)S(1)}, u32[]{:S(2)}, u32[]{:S(2)}) collective-permute-start(f32[9,4,512]{2,1,0:T(4,128)S(1)} %add.9), channel_id=1, source_target_pairs={{0,1},{1,0},{2,3},{3,2},{4,5},{5,4},{6,7},{7,6},{8,9},{9,8},{10,11... | collective-permute-start | bytes 221192 | tf_op jit(solution)/shard_map/ppermute | solution.py:203
  15.6 4.4 %collective-permute-start.2 = (f32[9,4,512]{2,1,0:T(4,128)S(1)}, f32[9,4,512]{2,1,0:T(4,128)S(1)}, u32[]{:S(2)}, u32[]{:S(2)}) collective-permute-start(f32[9,4,512]{2,1,0:T(4,128)S(1)} %add.9), channel_id=1, source_target_pairs={{0,2},{1,3},{2,0},{3,1},{4,6},{5,7},{6,4},{7,5},{8,10},{9,11},{10,... | collective-permute-start | bytes 221192 | tf_op jit(solution)/shard_map/ppermute | solution.py:203
  16.1 5.3 %collective-permute-start.3 = (f32[9,4,512]{2,1,0:T(4,128)S(1)}, f32[9,4,512]{2,1,0:T(4,128)S(1)}, u32[]{:S(2)}, u32[]{:S(2)}) collective-permute-start(f32[9,4,512]{2,1,0:T(4,128)S(1)} %add.9), channel_id=1, source_target_pairs={{0,3},{1,2},{2,1},{3,0},{4,7},{5,6},{6,5},{7,4},{8,11},{9,10},{10,... | collective-permute-start | bytes 221192 | tf_op jit(solution)/shard_map/ppermute | solution.py:203
  22.6 3.2 %collective-permute-start.4 = (f32[1,8320]{1,0:T(1,128)S(1)}, f32[1,8320]{1,0:T(1,128)S(1)}, u32[]{:S(2)}, u32[]{:S(2)}) collective-permute-start(f32[1,8320]{1,0:T(1,128)S(1)} %get-tuple-element.13.refs_0_), channel_id=1, source_target_pairs={{0,8},{8,0},{16,24},{24,16},{1,9},{9,1},{17,25},{25,17},{2,10},{10... | collective-permute-start | bytes 99848 | tf_op jit(solution)/shard_map/ppermute | solution.py:203
  22.6 4.0 %collective-permute-start.5 = (f32[1,8320]{1,0:T(1,128)S(1)}, f32[1,8320]{1,0:T(1,128)S(1)}, u32[]{:S(2)}, u32[]{:S(2)}) collective-permute-start(f32[1,8320]{1,0:T(1,128)S(1)} %get-tuple-element.13.refs_0_), channel_id=1, source_target_pairs={{0,16},{8,24},{16,0},{24,8},{1,17},{9,25},{17,1},{25,9},{2,18},{10... | collective-permute-start | bytes 99848 | tf_op jit(solution)/shard_map/ppermute | solution.py:203
  24.1 3.4 %collective-permute-start.6 = (f32[1,8320]{1,0:T(1,128)S(1)}, f32[1,8320]{1,0:T(1,128)S(1)}, u32[]{:S(2)}, u32[]{:S(2)}) collective-permute-start(f32[1,8320]{1,0:T(1,128)S(1)} %get-tuple-element.13.refs_0_), channel_id=1, source_target_pairs={{0,24},{8,16},{16,8},{24,0},{1,25},{9,17},{17,9},{25,1},{2,26},{10... | collective-permute-start | bytes 99848 | tf_op jit(solution)/shard_map/ppermute | solution.py:203

commit v5 on v4

--- a/solution.py
+++ b/solution.py
@@ -174,7 +174,7 @@
 
 def last_kernel(chunks, count, *refs):
     parts = refs[:count]
-    coef_ref, w_ref, s_ref, y_ref, new_ref, grad_ref = refs[count:]
+    coef_ref, w_ref, s_ref, y_ref, new_hbm, grad_hbm, new_ref, grad_ref, sem = refs[count:]
     both = 2 * HIST
     width = w_ref.shape[1]
     step = width // chunks
@@ -190,12 +190,18 @@
     coef = jnp.sum(coef_ref[:both, :] * dots, axis=1, keepdims=True)
     for c in range(chunks):
         cut = pl.ds(c * step, step)
-        weights = w_ref[:, cut]
-        gradient = weights + penalty * summed(cut)
-        grad_ref[:, cut] = gradient
+        grad_ref[:, cut] = w_ref[:, cut] + penalty * summed(cut)
+    copies = [pltpu.make_async_copy(grad_ref, grad_hbm, sem.at[0])]
+    copies[0].start()
+    for c in range(chunks):
+        cut = pl.ds(c * step, step)
         mixed = coef[:HIST] * s_ref[:, cut] + coef[HIST:] * y_ref[:, cut]
-        turn = gamma * gradient + jnp.sum(mixed, axis=0, keepdims=True)
-        new_ref[:, cut] = weights - step_length * turn
+        turn = gamma * grad_ref[:, cut] + jnp.sum(mixed, axis=0, keepdims=True)
+        new_ref[:, cut] = w_ref[:, cut] - step_length * turn
+    copies.append(pltpu.make_async_copy(new_ref, new_hbm, sem.at[1]))
+    copies[1].start()
+    for copy in copies:
+        copy.wait()
 
 
 def hop(values, axis, bit):
@@ -272,8 +278,13 @@
     new_w, grad = pl.pallas_call(
         lambda *refs: last_kernel(chunks, len(parts), *refs),
         in_specs=[VM] * (len(parts) + 4),
-        out_specs=[VM] * 2,
+        out_specs=[HBM] * 2,
         out_shape=[jax.ShapeDtypeStruct((1, width), f32)] * 2,
+        scratch_shapes=[
+            pltpu.VMEM((1, width), f32),
+            pltpu.VMEM((1, width), f32),
+            pltpu.SemaphoreType.DMA((2,)),
+        ],
         compiler_params=SMALL_GRANT,
         name="direction_and_update",
     )(*parts, coefs, w_in, s_in, y_in)

time: 28.5 us -> 28.5 us (level)
  no operation moved by 1% of the time
where the time goes in v5:
time: 28.5 us; the launch traced here: 28.4 us
  waiting for transfers between devices  9.58 us (34%)
  starting transfers between devices  9.55 us (34%)
  Pallas kernels  7.84 us (28%)
  between operations  1.33 us (5%)
    ppermute x7, waiting for transfers between devices, hop(): return lax.ppermute(values, axis, [(k, k ^ bit) for k in range(size)])  9.58 us
    ppermute x7, starting transfers between devices, hop(): return lax.ppermute(values, axis, [(k, k ^ bit) for k in range(size)])  9.55 us
    pallas_call x1, Pallas kernels, body(): pl.pallas_call(lambda *refs: first_kernel(blocks, *refs), in_specs=[SM] +...  5.1 us
    pallas_call x1, Pallas kernels, body(): pl.pallas_call(lambda *refs: second_kernel(chunks, *refs), in_specs=[VM]...  1.21 us
    pallas_call x1, Pallas kernels, body(): pl.pallas_call(lambda *refs: last_kernel(chunks, len(parts), *refs), in_s...  0.88 us
    pallas_call x1, Pallas kernels, body(): pl.pallas_call(solve_kernel, in_specs=[SM, VM], out_specs=VM, out_shape=p...  0.65 us
  transfers between devices with their start and end apart: 7, of which 6 were waited for; matrix products, arithmetic and copies ran while one was open for 0% of the time, Pallas kernels for 2%

profile of v5, /device:TPU:0, one launch (start us, length us, event | category | flops | bytes accessed | tf_op | source)
XLA Modules:
  0.0 28.4 jit_solution(7562610274029816987)
XLA Ops:
  0.6 0.0 copy-start
  0.6 5.1 %load_and_project.1 = (f32[9,4,512]{2,1,0:T(4,128)S(1)}, bf16[512,8192]{1,0:T(8,128)(2,1)S(1)}, f32[1,8192]{1,0:T(1,128)S(1)}, f32[16,8192]{1,0:T(8,128)S(1)}, f32[16,8192]{1,0:T(8,128)S(1)}) custom-call(s32[1]{0:T(128)} %bitcast.refs_0_, bf16[512,8192]{1,0:T(8,128)(2,1)} %refs_1_.1, f32[1,8192]{1,0:T(1,128)} %bitcast.6, f32[16,8192]{1,0:T(8,128)} %refs_3_.1, ...), custom_call_target="tpu_custom_call" | custom-call | tf_op jit(solution)/shard_map/load_and_project/pallas_call | solution.py:219
  5.8 4.1 %collective-permute-start = (f32[9,4,512]{2,1,0:T(4,128)S(1)}, f32[9,4,512]{2,1,0:T(4,128)S(1)}, u32[]{:S(2)}, u32[]{:S(2)}) collective-permute-start(f32[9,4,512]{2,1,0:T(4,128)S(1)} %get-tuple-element.12), channel_id=1, source_target_pairs={{0,4},{1,5},{2,6},{3,7},{4,0},{5,1},{6,2},{7,3},{8,12},{9,13},{10,... | collective-permute-start | bytes 221192 | tf_op jit(solution)/shard_map/ppermute | solution.py:209
  9.9 3.9 %collective-permute-done = f32[9,4,512]{2,1,0:T(4,128)S(1)} collective-permute-done((f32[9,4,512]{2,1,0:T(4,128)S(1)}, f32[9,4,512]{2,1,0:T(4,128)S(1)}, u32[]{:S(2)}, u32[]{:S(2)}) %collective-permute-start) | collective-permute-done | bytes 73760 | tf_op jit(solution)/shard_map/ppermute | solution.py:209
  13.8 1.8 %collective-permute-start.1 = (f32[9,4,512]{2,1,0:T(4,128)S(1)}, f32[9,4,512]{2,1,0:T(4,128)S(1)}, u32[]{:S(2)}, u32[]{:S(2)}) collective-permute-start(f32[9,4,512]{2,1,0:T(4,128)S(1)} %add.9), channel_id=1, source_target_pairs={{0,1},{1,0},{2,3},{3,2},{4,5},{5,4},{6,7},{7,6},{8,9},{9,8},{10,11... | collective-permute-start | bytes 221192 | tf_op jit(solution)/shard_map/ppermute | solution.py:209
  15.6 0.5 %collective-permute-start.2 = (f32[9,4,512]{2,1,0:T(4,128)S(1)}, f32[9,4,512]{2,1,0:T(4,128)S(1)}, u32[]{:S(2)}, u32[]{:S(2)}) collective-permute-start(f32[9,4,512]{2,1,0:T(4,128)S(1)} %add.9), channel_id=1, source_target_pairs={{0,2},{1,3},{2,0},{3,1},{4,6},{5,7},{6,4},{7,5},{8,10},{9,11},{10,... | collective-permute-start | bytes 221192 | tf_op jit(solution)/shard_map/ppermute | solution.py:209
  16.1 1.3 %collective-permute-start.3 = (f32[9,4,512]{2,1,0:T(4,128)S(1)}, f32[9,4,512]{2,1,0:T(4,128)S(1)}, u32[]{:S(2)}, u32[]{:S(2)}) collective-permute-start(f32[9,4,512]{2,1,0:T(4,128)S(1)} %add.9), channel_id=1, source_target_pairs={{0,3},{1,2},{2,1},{3,0},{4,7},{5,6},{6,5},{7,4},{8,11},{9,10},{10,... | collective-permute-start | bytes 221192 | tf_op jit(solution)/shard_map/ppermute | solution.py:209
  17.4 0.9 %collective-permute-done.1 = f32[9,4,512]{2,1,0:T(4,128)S(1)} collective-permute-done((f32[9,4,512]{2,1,0:T(4,128)S(1)}, f32[9,4,512]{2,1,0:T(4,128)S(1)}, u32[]{:S(2)}, u32[]{:S(2)}) %collective-permute-start.1) | collective-permute-done | bytes 73760 | tf_op jit(solution)/shard_map/ppermute | solution.py:209
  18.3 1.6 %collective-permute-done.2 = f32[9,4,512]{2,1,0:T(4,128)S(1)} collective-permute-done((f32[9,4,512]{2,1,0:T(4,128)S(1)}, f32[9,4,512]{2,1,0:T(4,128)S(1)}, u32[]{:S(2)}, u32[]{:S(2)}) %collective-permute-start.2) | collective-permute-done | bytes 73760 | tf_op jit(solution)/shard_map/ppermute | solution.py:209
  20.0 1.4 %collective-permute-done.3 = f32[9,4,512]{2,1,0:T(4,128)S(1)} collective-permute-done((f32[9,4,512]{2,1,0:T(4,128)S(1)}, f32[9,4,512]{2,1,0:T(4,128)S(1)}, u32[]{:S(2)}, u32[]{:S(2)}) %collective-permute-start.3) | collective-permute-done | bytes 73760 | tf_op jit(solution)/shard_map/ppermute | solution.py:209
  21.4 0.0 copy-done
  21.4 1.2 %residual_and_gradient.1 = (f32[1,8320]{1,0:T(1,128)S(1)}, f32[4,512]{1,0:T(4,128)S(1)}) custom-call(bf16[512,8192]{1,0:T(8,128)(2,1)S(1)} %get-tuple-element.11.refs_0_, f32[9,4,512]{2,1,0:T(4,128)S(1)} %add.10.refs_1_, f32[9,4,512]{2,1,0:T(4,128)S(1)} %add.11.refs_2_, s32[1,512]{1,0:T(1,128)S(1)} %bitcast.5), custom_call_target="tpu_custom_call" | custom-call | tf_op jit(solution)/shard_map/residual_and_gradient/pallas_call | solution.py:253
  22.6 0.0 collective-permute-start.4
  22.6 1.6 %collective-permute-start.5 = (f32[1,8320]{1,0:T(1,128)S(1)}, f32[1,8320]{1,0:T(1,128)S(1)}, u32[]{:S(2)}, u32[]{:S(2)}) collective-permute-start(f32[1,8320]{1,0:T(1,128)S(1)} %get-tuple-element.13.refs_0_), channel_id=1, source_target_pairs={{0,16},{8,24},{16,0},{24,8},{1,17},{9,25},{17,1},{25,9},{2,18},{10... | collective-permute-start | bytes 99848 | tf_op jit(solution)/shard_map/ppermute | solution.py:209
  24.1 0.3 %collective-permute-start.6 = (f32[1,8320]{1,0:T(1,128)S(1)}, f32[1,8320]{1,0:T(1,128)S(1)}, u32[]{:S(2)}, u32[]{:S(2)}) collective-permute-start(f32[1,8320]{1,0:T(1,128)S(1)} %get-tuple-element.13.refs_0_), channel_id=1, source_target_pairs={{0,24},{8,16},{16,8},{24,0},{1,25},{9,17},{17,9},{25,1},{2,26},{10... | collective-permute-start | bytes 99848 | tf_op jit(solution)/shard_map/ppermute | solution.py:209
  25.1 0.7 %solve_history.1.refs_4_ = f32[40,128]{1,0:T(8,128)S(1)} custom-call(s32[1]{0:T(128)S(6)} %copy.8.counter, f32[4,512]{1,0:T(4,128)S(1)} %get-tuple-element.14.gram), custom_call_target="tpu_custom_call" | custom-call | tf_op jit(solution)/shard_map/solve_history/pallas_call | solution.py:262
  25.7 0.0 collective-permute-done.4.refs_1_
  25.7 0.8 %collective-permute-done.5.refs_2_ = f32[1,8320]{1,0:T(1,128)S(1)} collective-permute-done((f32[1,8320]{1,0:T(1,128)S(1)}, f32[1,8320]{1,0:T(1,128)S(1)}, u32[]{:S(2)}, u32[]{:S(2)}) %collective-permute-start.5) | collective-permute-done | bytes 33312 | tf_op jit(solution)/shard_map/ppermute | solution.py:209
  26.6 0.9 %collective-permute-done.6.refs_3_ = f32[1,8320]{1,0:T(1,128)S(1)} collective-permute-done((f32[1,8320]{1,0:T(1,128)S(1)}, f32[1,8320]{1,0:T(1,128)S(1)}, u32[]{:S(2)}, u32[]{:S(2)}) %collective-permute-start.6) | collective-permute-done | bytes 33312 | tf_op jit(solution)/shard_map/ppermute | solution.py:209
  27.5 0.9 %direction_and_update.1 = (f32[1,8192]{1,0:T(1,128)}, f32[1,8192]{1,0:T(1,128)}) custom-call(f32[1,8320]{1,0:T(1,128)S(1)} %get-tuple-element.13.refs_0_, f32[1,8320]{1,0:T(1,128)S(1)} %collective-permute-done.4.refs_1_, f32[1,8320]{1,0:T(1,128)S(1)} %collective-permute-done.5.refs_2_, f32[1,8320]{1,0:T(1,128)S(1)} %collective-permute-done.6.refs_3_, ...), custom_call_target="tpu_custom_call" | custom-call | tf_op jit(solution)/shard_map/direction_and_update/pallas_call | solution.py:278
  (3 shorter events, 0.1 us)
Async XLA Ops:
  0.6 20.7 %copy-start = (s32[512]{0:T(512)S(1)}, s32[512]{0:T(512)}, u32[]{:S(2)}) copy-start(s32[512]{0:T(512)} %param.7) | copy-start | bytes 6148
  5.8 8.0 %collective-permute-start = (f32[9,4,512]{2,1,0:T(4,128)S(1)}, f32[9,4,512]{2,1,0:T(4,128)S(1)}, u32[]{:S(2)}, u32[]{:S(2)}) collective-permute-start(f32[9,4,512]{2,1,0:T(4,128)S(1)} %get-tuple-element.12), channel_id=1, source_target_pairs={{0,4},{1,5},{2,6},{3,7},{4,0},{5,1},{6,2},{7,3},{8,12},{9,13},{10,... | collective-permute-start | bytes 221192 | tf_op jit(solution)/shard_map/ppermute | solution.py:209
  13.8 4.5 %collective-permute-start.1 = (f32[9,4,512]{2,1,0:T(4,128)S(1)}, f32[9,4,512]{2,1,0:T(4,128)S(1)}, u32[]{:S(2)}, u32[]{:S(2)}) collective-permute-start(f32[9,4,512]{2,1,0:T(4,128)S(1)} %add.9), channel_id=1, source_target_pairs={{0,1},{1,0},{2,3},{3,2},{4,5},{5,4},{6,7},{7,6},{8,9},{9,8},{10,11... | collective-permute-start | bytes 221192 | tf_op jit(solution)/shard_map/ppermute | solution.py:209
  15.6 4.4 %collective-permute-start.2 = (f32[9,4,512]{2,1,0:T(4,128)S(1)}, f32[9,4,512]{2,1,0:T(4,128)S(1)}, u32[]{:S(2)}, u32[]{:S(2)}) collective-permute-start(f32[9,4,512]{2,1,0:T(4,128)S(1)} %add.9), channel_id=1, source_target_pairs={{0,2},{1,3},{2,0},{3,1},{4,6},{5,7},{6,4},{7,5},{8,10},{9,11},{10,... | collective-permute-start | bytes 221192 | tf_op jit(solution)/shard_map/ppermute | solution.py:209
  16.1 5.3 %collective-permute-start.3 = (f32[9,4,512]{2,1,0:T(4,128)S(1)}, f32[9,4,512]{2,1,0:T(4,128)S(1)}, u32[]{:S(2)}, u32[]{:S(2)}) collective-permute-start(f32[9,4,512]{2,1,0:T(4,128)S(1)} %add.9), channel_id=1, source_target_pairs={{0,3},{1,2},{2,1},{3,0},{4,7},{5,6},{6,5},{7,4},{8,11},{9,10},{10,... | collective-permute-start | bytes 221192 | tf_op jit(solution)/shard_map/ppermute | solution.py:209
  22.6 3.2 %collective-permute-start.4 = (f32[1,8320]{1,0:T(1,128)S(1)}, f32[1,8320]{1,0:T(1,128)S(1)}, u32[]{:S(2)}, u32[]{:S(2)}) collective-permute-start(f32[1,8320]{1,0:T(1,128)S(1)} %get-tuple-element.13.refs_0_), channel_id=1, source_target_pairs={{0,8},{8,0},{16,24},{24,16},{1,9},{9,1},{17,25},{25,17},{2,10},{10... | collective-permute-start | bytes 99848 | tf_op jit(solution)/shard_map/ppermute | solution.py:209
  22.6 4.0 %collective-permute-start.5 = (f32[1,8320]{1,0:T(1,128)S(1)}, f32[1,8320]{1,0:T(1,128)S(1)}, u32[]{:S(2)}, u32[]{:S(2)}) collective-permute-start(f32[1,8320]{1,0:T(1,128)S(1)} %get-tuple-element.13.refs_0_), channel_id=1, source_target_pairs={{0,16},{8,24},{16,0},{24,8},{1,17},{9,25},{17,1},{25,9},{2,18},{10... | collective-permute-start | bytes 99848 | tf_op jit(solution)/shard_map/ppermute | solution.py:209
  24.1 3.4 %collective-permute-start.6 = (f32[1,8320]{1,0:T(1,128)S(1)}, f32[1,8320]{1,0:T(1,128)S(1)}, u32[]{:S(2)}, u32[]{:S(2)}) collective-permute-start(f32[1,8320]{1,0:T(1,128)S(1)} %get-tuple-element.13.refs_0_), channel_id=1, source_target_pairs={{0,24},{8,16},{16,8},{24,0},{1,25},{9,17},{17,9},{25,1},{2,26},{10... | collective-permute-start | bytes 99848 | tf_op jit(solution)/shard_map/ppermute | solution.py:209
